TPU v7x, 8 devices: a whole 2x2x1 slice. The times are simulated.
8 devices in a mesh: data: 1 (over z), tp: 2 (over y), ep: 4 (over x, core).
Axes of the slice: x: 2, y: 2, z: 1, core: 2. Of those that a mesh axis runs over, the one named last changes fastest.
Arguments:
- tokens_a: bfloat16 [1024, 1536], P(('data', 'ep', 'tp'))
- tokens_b: bfloat16 [1024, 1536], P(('data', 'ep', 'tp'))
- experts_a: int32 [1024, 6], P(('data', 'ep', 'tp'))
- experts_b: int32 [1024, 6], P(('data', 'ep', 'tp'))
- gates_a: float32 [1024, 6], P(('data', 'ep', 'tp'))
- gates_b: float32 [1024, 6], P(('data', 'ep', 'tp'))
- slots_a: int32 [1024, 6], P(('data', 'ep', 'tp'))
- slots_b: int32 [1024, 6], P(('data', 'ep', 'tp'))
- shared_w1: bfloat16 [1536, 1024], P(None, 'tp')
- shared_w3: bfloat16 [1536, 1024], P(None, 'tp')
- shared_w2: bfloat16 [1024, 1536], P('tp')
- routed_w1: bfloat16 [64, 1536, 512], P('ep')
- routed_w3: bfloat16 [64, 1536, 512], P('ep')
- routed_w2: bfloat16 [64, 512, 1536], P('ep')
Outputs:
- output 1: bfloat16 [1024, 1536], P(('data', 'ep', 'tp'))
- output 2: bfloat16 [1024, 1536], P(('data', 'ep', 'tp'))
All inputs are finite; a program needn't handle non-finite values.
Results may differ from a plain program's by a relative error of at most 0.00605838.
Values are sent between devices in bfloat16 or wider.
A program may use at most 1 GiB of HBM per device.

v0:
```python
import jax
import jax.numpy as jnp
from jax import lax
from jax.sharding import PartitionSpec as P


def capacity_rows(tok_local, top_k, num_experts):
    return max(4, (2 * tok_local * top_k) // num_experts)


def swiglu_rows(rows, w_in, w_gate, w_out):
    proj_in = jnp.dot(rows, w_in, preferred_element_type=jnp.float32)
    proj_gate = jnp.dot(rows, w_gate, preferred_element_type=jnp.float32)
    hidden = (jax.nn.silu(proj_in) * proj_gate).astype(jnp.bfloat16)
    return jnp.dot(hidden, w_out, preferred_element_type=jnp.float32)


def solution(mesh):
    ep_size = mesh.shape['ep']
    tok_spec = P(('data', 'ep', 'tp'), None)
    in_specs = (tok_spec,) * 8 + (P(None, 'tp'), P(None, 'tp'), P('tp', None), P('ep', None, None), P('ep', None, None), P('ep', None, None))

    def shared_path(x_local, shared_w1, shared_w3, shared_w2):
        gathered = lax.all_gather(x_local, 'tp', axis=0, tiled=True)
        partial_sum = swiglu_rows(gathered, shared_w1, shared_w3, shared_w2)
        return lax.psum_scatter(partial_sum, 'tp', scatter_dimension=0, tiled=True)

    def routed_path(x_local, expert_ids, gate_vals, slot_ids, routed_w1, routed_w3, routed_w2):
        tok_local, top_k = expert_ids.shape
        local_experts, model_dim, expert_ff = routed_w1.shape
        cap_rows = capacity_rows(tok_local, top_k, local_experts * ep_size)
        num_rows = local_experts * ep_size * cap_rows
        dest_rank = expert_ids // local_experts
        local_id = expert_ids % local_experts
        keep_mask = slot_ids >= 0
        row_ids = jnp.where(keep_mask, (local_id * ep_size + dest_rank) * cap_rows + slot_ids, -1)
        place_mat = jnp.any(row_ids[:, :, None] == jnp.arange(num_rows)[None, None, :], axis=1).astype(jnp.bfloat16)
        send_rows = jnp.einsum('tr,td->rd', place_mat, x_local, preferred_element_type=jnp.float32).astype(jnp.bfloat16)
        recv_rows = lax.all_to_all(send_rows.reshape(local_experts, ep_size, cap_rows, model_dim), 'ep', 1, 1, tiled=True)
        recv_rows = recv_rows.reshape(local_experts, ep_size * cap_rows, model_dim)
        proj_in = jnp.einsum('erd,edf->erf', recv_rows, routed_w1, preferred_element_type=jnp.float32)
        proj_gate = jnp.einsum('erd,edf->erf', recv_rows, routed_w3, preferred_element_type=jnp.float32)
        hidden = (jax.nn.silu(proj_in) * proj_gate).astype(jnp.bfloat16)
        expert_out = jnp.einsum('erf,efd->erd', hidden, routed_w2, preferred_element_type=jnp.float32).astype(jnp.bfloat16)
        back_rows = lax.all_to_all(expert_out.reshape(local_experts, ep_size, cap_rows, model_dim), 'ep', 1, 1, tiled=True)
        picked = jnp.take(back_rows.reshape(num_rows, model_dim), jnp.maximum(row_ids, 0), axis=0)
        weights = jnp.where(keep_mask, gate_vals, 0.0)
        return jnp.sum(picked.astype(jnp.float32) * weights[:, :, None], axis=1)

    def layer_local(tokens_a, tokens_b, experts_a, experts_b, gates_a, gates_b, slots_a, slots_b, shared_w1, shared_w3, shared_w2, routed_w1, routed_w3, routed_w2):
        def one_microbatch(x_local, expert_ids, gate_vals, slot_ids):
            shared_out = shared_path(x_local, shared_w1, shared_w3, shared_w2)
            routed_out = routed_path(x_local, expert_ids, gate_vals, slot_ids, routed_w1, routed_w3, routed_w2)
            return (x_local.astype(jnp.float32) + shared_out + routed_out).astype(jnp.bfloat16)
        out_a = one_microbatch(tokens_a, experts_a, gates_a, slots_a)
        out_b = one_microbatch(tokens_b, experts_b, gates_b, slots_b)
        return (out_a, out_b)

    return jax.shard_map(layer_local, mesh=mesh, in_specs=in_specs, out_specs=(tok_spec, tok_spec), check_vma=False)
```

profile of v0, /device:TPU:0, one launch (start us, length us, event | category | flops | bytes accessed | tf_op | source)
XLA Modules:
  0.0 288.2 jit_solution(11869512566651956062)
XLA Ops:
  14.4 5.1 %all-to-all-start.2 = ((bf16[16,4,24,1536]{3,2,0,1:T(8,128)(2,1)}), bf16[16,4,24,1536]{3,2,0,1:T(8,128)(2,1)}, u32[]{:S(2)}, u32[]{:S(2)}) async-start(bf16[16,4,24,1536]{3,2,0,1:T(8,128)(2,1)} %copy.54), calls=%async_computation.4 | async-start | bytes 9437184 | tf_op jit(solution)/shard_map/all_to_all | solution.py:39
  19.6 13.7 %all_gather.7 = bf16[256,1536]{1,0:T(8,128)(2,1)S(1)} all-gather(bf16[128,1536]{1,0:T(8,128)(2,1)S(1)} %copy-done.5), channel_id=1, replica_groups=mesh['data'=1,'tp'=2,'ep'=4] {'tp'}, dimensions={0}, use_global_device_ids=true | all-gather | bytes 1179648 | tf_op jit(solution)/shard_map/all_gather | solution.py:24
  35.6 4.0 %fusion.6 = f32[256,1536]{1,0:T(8,128)} fusion(bf16[512,1536]{1,0:T(8,128)(2,1)S(1)} %copy-done, bf16[256,1536]{1,0:T(8,128)(2,1)} %copy-done.7, bf16[1536,512]{1,0:T(8,128)(2,1)} %param.25, f32[256,512]{1,0:T(8,128)} %fusion.46), kind=kOutput, calls=%fused_computation.20 | convolution fusion | flops 806092800 | bytes 6029312 | tf_op jit(solution)/shard_map/dot_general | solution.py:15
  46.0 28.0 %all-to-all-done.2 = bf16[16,4,24,1536]{3,2,0,1:T(8,128)(2,1)} async-done(((bf16[16,4,24,1536]{3,2,0,1:T(8,128)(2,1)}), bf16[16,4,24,1536]{3,2,0,1:T(8,128)(2,1)}, u32[]{:S(2)}, u32[]{:S(2)}) %all-to-all-start.2) | async-done | bytes 4718624 | tf_op jit(solution)/shard_map/all_to_all | solution.py:39
  74.0 5.2 %all-to-all-start = ((bf16[16,4,24,1536]{3,2,0,1:T(8,128)(2,1)}), bf16[16,4,24,1536]{3,2,0,1:T(8,128)(2,1)}, u32[]{:S(2)}, u32[]{:S(2)}) async-start(bf16[16,4,24,1536]{3,2,0,1:T(8,128)(2,1)} %copy.47), calls=%async_computation.1 | async-start | bytes 9437184 | tf_op jit(solution)/shard_map/all_to_all | solution.py:39
  84.2 14.0 %fusion.47 = f32[16,96,512]{2,1,0:T(8,128)} fusion(bf16[16,96,1536]{2,1,0:T(8,128)(2,1)S(1)} %bitcast.34, bf16[16,1536,512]{2,1,0:T(8,128)(2,1)} %param.27), kind=kOutput, calls=%fused_computation.83 | convolution fusion | flops 2415919104 | bytes 33030144 | tf_op jit(solution)/shard_map/erd,edf->erf/dot_general | solution.py:41
  98.2 26.7 %convolution_convert_fusion.2 = bf16[16,96,1536]{2,1,0:T(8,128)(2,1)} fusion(bf16[16,512,1536]{2,1,0:T(8,128)(2,1)} %param.29, f32[16,96,512]{2,1,0:T(8,128)} %fusion.47, bf16[16,96,1536]{2,1,0:T(8,128)(2,1)} %bitcast.35, bf16[16,1536,512]{2,1,0:T(8,128)(2,1)} %param.28), kind=kOutput, calls=%fused_computation.10 | convolution fusion | flops 4838916096 | bytes 62914560 | tf_op jit(solution)/shard_map/erf,efd->erd/dot_general | solution.py:44
  124.9 5.0 %copy.56 = bf16[16,4,24,1536]{3,2,0,1:T(8,128)(2,1)} copy(bf16[16,4,24,1536]{3,2,1,0:T(8,128)(2,1)} %bitcast.40) | data formatting | bytes 9437184 | tf_op jit(solution)/shard_map/reshape | solution.py:45
  132.5 5.0 %all-to-all-start.3 = ((bf16[16,4,24,1536]{3,2,0,1:T(8,128)(2,1)}), bf16[16,4,24,1536]{3,2,0,1:T(8,128)(2,1)}, u32[]{:S(2)}, u32[]{:S(2)}) async-start(bf16[16,4,24,1536]{3,2,0,1:T(8,128)(2,1)} %copy.56), calls=%async_computation.5 | async-start | bytes 9437184 | tf_op jit(solution)/shard_map/all_to_all | solution.py:45
  142.5 14.0 %fusion.45 = f32[16,96,512]{2,1,0:T(8,128)} fusion(bf16[16,96,1536]{2,1,0:T(8,128)(2,1)S(1)} %bitcast.36, bf16[16,1536,512]{2,1,0:T(8,128)(2,1)} %param.27), kind=kOutput, calls=%fused_computation.81 | convolution fusion | flops 2415919104 | bytes 33030144 | tf_op jit(solution)/shard_map/erd,edf->erf/dot_general | solution.py:41
  156.5 26.7 %convolution_convert_fusion.3 = bf16[16,96,1536]{2,1,0:T(8,128)(2,1)} fusion(bf16[16,512,1536]{2,1,0:T(8,128)(2,1)} %param.29, f32[16,96,512]{2,1,0:T(8,128)} %fusion.45, bf16[16,96,1536]{2,1,0:T(8,128)(2,1)} %bitcast.37, bf16[16,1536,512]{2,1,0:T(8,128)(2,1)} %param.28), kind=kOutput, calls=%fused_computation.11 | convolution fusion | flops 4838916096 | bytes 62914560 | tf_op jit(solution)/shard_map/erf,efd->erd/dot_general | solution.py:44
  183.2 5.0 %copy.49 = bf16[16,4,24,1536]{3,2,0,1:T(8,128)(2,1)} copy(bf16[16,4,24,1536]{3,2,1,0:T(8,128)(2,1)} %bitcast.41) | data formatting | bytes 9437184 | tf_op jit(solution)/shard_map/reshape | solution.py:45
  191.0 5.2 %all-to-all-start.1 = ((bf16[16,4,24,1536]{3,2,0,1:T(8,128)(2,1)}), bf16[16,4,24,1536]{3,2,0,1:T(8,128)(2,1)}, u32[]{:S(2)}, u32[]{:S(2)}) async-start(bf16[16,4,24,1536]{3,2,0,1:T(8,128)(2,1)} %copy.49), calls=%async_computation.2 | async-start | bytes 9437184 | tf_op jit(solution)/shard_map/all_to_all | solution.py:45
  196.2 12.7 %all_gather.6 = bf16[256,1536]{1,0:T(8,128)(2,1)S(1)} all-gather(bf16[128,1536]{1,0:T(8,128)(2,1)} %param.16), channel_id=1, replica_groups=mesh['data'=1,'tp'=2,'ep'=4] {'tp'}, dimensions={0}, use_global_device_ids=true | all-gather | bytes 1179648 | tf_op jit(solution)/shard_map/all_gather | solution.py:24
  211.2 4.0 %fusion.7 = f32[256,1536]{1,0:T(8,128)} fusion(bf16[512,1536]{1,0:T(8,128)(2,1)S(1)} %copy-done, bf16[256,1536]{1,0:T(8,128)(2,1)} %copy-done.8, bf16[1536,512]{1,0:T(8,128)(2,1)} %param.25, f32[256,512]{1,0:T(8,128)} %fusion.44), kind=kOutput, calls=%fused_computation.21 | convolution fusion | flops 806092800 | bytes 6029312 | tf_op jit(solution)/shard_map/dot_general | solution.py:15
  216.4 5.0 %copy.57 = bf16[16,4,24,1536]{3,2,1,0:T(8,128)(2,1)} copy(bf16[16,4,24,1536]{3,2,0,1:T(8,128)(2,1)} %all-to-all-done.3) | data formatting | bytes 9437184 | tf_op jit(solution)/shard_map/all_to_all | solution.py:45
  221.4 8.8 %gather_fusion.1 = bf16[768,1536]{1,0:T(8,128)(2,1)} fusion(bf16[1536,1536]{1,0:T(8,128)(2,1)} %bitcast.32, s32[1024]{0:T(1024)S(1)} %pad_clamp_fusion), kind=kCustom, calls=%fused_computation.1.clone | custom fusion | bytes 4721664 | tf_op jit(solution)/shard_map/jit(_take)/gather | solution.py:46
  230.2 4.9 %reshape.72 = bf16[128,6,1536]{2,1,0:T(8,128)(2,1)} reshape(bf16[768,1536]{1,0:T(8,128)(2,1)} %gather_fusion.1) | data formatting | bytes 4718592 | tf_op jit(solution)/shard_map/jit(_take)/gather | solution.py:46
  235.1 14.5 %all-to-all-done.1 = bf16[16,4,24,1536]{3,2,0,1:T(8,128)(2,1)} async-done(((bf16[16,4,24,1536]{3,2,0,1:T(8,128)(2,1)}), bf16[16,4,24,1536]{3,2,0,1:T(8,128)(2,1)}, u32[]{:S(2)}, u32[]{:S(2)}) %all-to-all-start.1) | async-done | bytes 4718624 | tf_op jit(solution)/shard_map/all_to_all | solution.py:45
  249.7 5.0 %copy.50 = bf16[16,4,24,1536]{3,2,1,0:T(8,128)(2,1)} copy(bf16[16,4,24,1536]{3,2,0,1:T(8,128)(2,1)} %all-to-all-done.1) | data formatting | bytes 9437184 | tf_op jit(solution)/shard_map/all_to_all | solution.py:45
  254.7 8.9 %gather_fusion = bf16[768,1536]{1,0:T(8,128)(2,1)} fusion(bf16[1536,1536]{1,0:T(8,128)(2,1)} %bitcast.33, s32[1024]{0:T(1024)S(1)} %pad_clamp_fusion.1), kind=kCustom, calls=%fused_computation.clone | custom fusion | bytes 4721664 | tf_op jit(solution)/shard_map/jit(_take)/gather | solution.py:46
  263.5 4.9 %reshape.68 = bf16[128,6,1536]{2,1,0:T(8,128)(2,1)} reshape(bf16[768,1536]{1,0:T(8,128)(2,1)} %gather_fusion) | data formatting | bytes 4718592 | tf_op jit(solution)/shard_map/jit(_take)/gather | solution.py:46
  268.4 5.6 %multiply_reduce_fusion = f32[128,1536]{1,0:T(8,128)} fusion(bf16[128,6,1536]{2,1,0:T(8,128)(2,1)} %reshape.72, f32[128,6]{1,0:T(8,128)S(1)} %copy.59, pred[128,6]{1,0:T(8,128)(4,1)S(1)} %copy.53), kind=kLoop, calls=%fused_computation.4 | loop fusion | flops 4521984 | bytes 3149568 | tf_op jit(solution)/shard_map/reduce_sum | solution.py:48
  274.0 3.1 %multiply_reduce_fusion.1 = f32[128,1536]{1,0:T(8,128)S(1)} fusion(bf16[128,6,1536]{2,1,0:T(8,128)(2,1)S(1)} %copy-done.3, f32[128,6]{1,0:T(8,128)S(1)} %copy.52, pred[128,6]{1,0:T(8,128)(4,1)S(1)} %copy.46), kind=kLoop, calls=%fused_computation.5 | loop fusion | flops 4521984 | bytes 3149568 | tf_op jit(solution)/shard_map/reduce_sum | solution.py:48
  (68 shorter events, 39.0 us)
Async XLA Ops:
  7.2 28.4 %copy-start = (bf16[512,1536]{1,0:T(8,128)(2,1)S(1)}, bf16[512,1536]{1,0:T(8,128)(2,1)}, u32[]{:S(2)}) copy-start(bf16[512,1536]{1,0:T(8,128)(2,1)} %param.26) | copy-start | bytes 4718596
  14.4 5.1 %copy-start.5 = (bf16[128,1536]{1,0:T(8,128)(2,1)S(1)}, bf16[128,1536]{1,0:T(8,128)(2,1)}, u32[]{:S(2)}) copy-start(bf16[128,1536]{1,0:T(8,128)(2,1)} %param.17) | copy-start | bytes 1179652
  14.4 19.8 %copy-start.4 = (bf16[1536,512]{1,0:T(8,128)(2,1)S(1)}, bf16[1536,512]{1,0:T(8,128)(2,1)}, u32[]{:S(2)}) copy-start(bf16[1536,512]{1,0:T(8,128)(2,1)} %param.24) | copy-start | bytes 4718596
  14.4 59.6 %all-to-all-start.2 = ((bf16[16,4,24,1536]{3,2,0,1:T(8,128)(2,1)}), bf16[16,4,24,1536]{3,2,0,1:T(8,128)(2,1)}, u32[]{:S(2)}, u32[]{:S(2)}) async-start(bf16[16,4,24,1536]{3,2,0,1:T(8,128)(2,1)} %copy.54), calls=%async_computation.4 | async-start | bytes 9437184 | tf_op jit(solution)/shard_map/all_to_all | solution.py:39
  19.5 257.6 %reduce-scatter.5.cloned.1.call-start = ((), (), s32[]{:S(2)}) async-start(), calls=%async_computation.7 | async-start | bytes 2359296 | tf_op jit(solution)/shard_map/reduce_scatter | solution.py:26
  33.3 0.9 copy-start.7
  35.6 4.1 %copy-start.10 = (s32[128,6]{0,1:T(8,128)S(1)}, s32[128,6]{0,1:T(8,128)}, u32[]{:S(2)}) copy-start(s32[128,6]{0,1:T(8,128)} %param.22) | copy-start | bytes 9220
  35.6 4.1 %copy-start.13 = (s32[128,6]{0,1:T(8,128)S(1)}, s32[128,6]{0,1:T(8,128)}, u32[]{:S(2)}) copy-start(s32[128,6]{0,1:T(8,128)} %param.18) | copy-start | bytes 9220
  74.0 58.5 %all-to-all-start = ((bf16[16,4,24,1536]{3,2,0,1:T(8,128)(2,1)}), bf16[16,4,24,1536]{3,2,0,1:T(8,128)(2,1)}, u32[]{:S(2)}, u32[]{:S(2)}) async-start(bf16[16,4,24,1536]{3,2,0,1:T(8,128)(2,1)} %copy.47), calls=%async_computation.1 | async-start | bytes 9437184 | tf_op jit(solution)/shard_map/all_to_all | solution.py:39
  82.0 2.2 copy-start.1
  132.5 58.5 %all-to-all-start.3 = ((bf16[16,4,24,1536]{3,2,0,1:T(8,128)(2,1)}), bf16[16,4,24,1536]{3,2,0,1:T(8,128)(2,1)}, u32[]{:S(2)}, u32[]{:S(2)}) async-start(bf16[16,4,24,1536]{3,2,0,1:T(8,128)(2,1)} %copy.56), calls=%async_computation.5 | async-start | bytes 9437184 | tf_op jit(solution)/shard_map/all_to_all | solution.py:45
  140.3 2.2 copy-start.2
  191.0 58.7 %all-to-all-start.1 = ((bf16[16,4,24,1536]{3,2,0,1:T(8,128)(2,1)}), bf16[16,4,24,1536]{3,2,0,1:T(8,128)(2,1)}, u32[]{:S(2)}, u32[]{:S(2)}) async-start(bf16[16,4,24,1536]{3,2,0,1:T(8,128)(2,1)} %copy.49), calls=%async_computation.2 | async-start | bytes 9437184 | tf_op jit(solution)/shard_map/all_to_all | solution.py:45
  196.1 83.2 %reduce-scatter.3.cloned.1.call-start = ((), (), s32[]{:S(2)}) async-start(), calls=%async_computation.6 | async-start | bytes 2359296 | tf_op jit(solution)/shard_map/reduce_scatter | solution.py:26
  208.9 0.9 copy-start.8
  211.2 4.4 %copy-start.14 = (pred[128,6]{0,1:T(8,128)(4,1)S(1)}, pred[128,6]{0,1:T(8,128)(4,1)}, u32[]{:S(2)}) copy-start(pred[128,6]{0,1:T(8,128)(4,1)} %get-tuple-element.3) | copy-start | bytes 2308
  211.2 4.5 %copy-start.9 = (s32[128,6]{0,1:T(8,128)S(1)}, s32[128,6]{0,1:T(8,128)}, u32[]{:S(2)}) copy-start(s32[128,6]{0,1:T(8,128)} %param.23) | copy-start | bytes 9220
  211.2 4.5 %copy-start.11 = (f32[128,6]{0,1:T(8,128)S(1)}, f32[128,6]{0,1:T(8,128)}, u32[]{:S(2)}) copy-start(f32[128,6]{0,1:T(8,128)} %param.21) | copy-start | bytes 9220
  211.2 4.9 %copy-start.15 = (pred[128,6]{0,1:T(8,128)(4,1)S(1)}, pred[128,6]{0,1:T(8,128)(4,1)}, u32[]{:S(2)}) copy-start(pred[128,6]{0,1:T(8,128)(4,1)} %get-tuple-element.5) | copy-start | bytes 2308
  211.2 5.0 %copy-start.12 = (f32[128,6]{0,1:T(8,128)S(1)}, f32[128,6]{0,1:T(8,128)}, u32[]{:S(2)}) copy-start(f32[128,6]{0,1:T(8,128)} %param.20) | copy-start | bytes 9220
  268.4 5.6 %copy-start.3 = (bf16[128,6,1536]{2,1,0:T(8,128)(2,1)S(1)}, bf16[128,6,1536]{2,1,0:T(8,128)(2,1)}, u32[]{:S(2)}) copy-start(bf16[128,6,1536]{2,1,0:T(8,128)(2,1)} %reshape.68) | copy-start | bytes 7077892
  274.0 5.4 %copy-start.6 = (bf16[128,1536]{1,0:T(8,128)(2,1)S(1)}, bf16[128,1536]{1,0:T(8,128)(2,1)}, u32[]{:S(2)}) copy-start(bf16[128,1536]{1,0:T(8,128)(2,1)} %param.16) | copy-start | bytes 1179652
Sparse Core Ops, SparseCore 0:
  39.7 24.5 reduce-scatter.4
  215.4 24.6 reduce-scatter.2
where the time goes:
time: 289 us; the launch traced here: 288 us
  matrix products  97.1 us (34%)
  local copies, waits for them, and re-layouts  65.4 us (23%)
  waiting for transfers between devices  48.1 us (17%)
  blocking collectives  26.4 us (9%)
  starting transfers between devices  20.4 us (7%)
  other arithmetic  16.5 us (6%)
  between operations  14.3 us (5%)
    dot_general x2, matrix products, routed_path(): jnp.einsum('erf,efd->erd', hidden, routed_w2, preferred_element_type=jnp....  53.4 us
    all_to_all x2, waiting for transfers between devices, routed_path(): lax.all_to_all(send_rows.reshape(local_experts, ep_size, cap_rows, model_...  30.7 us
    dot_general x2, matrix products, routed_path(): jnp.einsum('erd,edf->erf', recv_rows, routed_w1, preferred_element_type=j...  28 us
    gather x4, local copies, waits for them, and re-layouts, routed_path(): jnp.take(back_rows.reshape(num_rows, model_dim), jnp.maximum(row_ids, 0),...  27.5 us
    all_gather x2, blocking collectives, shared_path(): gathered = lax.all_gather(x_local, 'tp', axis=0, tiled=True)  26.4 us
    all_to_all x2, waiting for transfers between devices, routed_path(): lax.all_to_all(expert_out.reshape(local_experts, ep_size, cap_rows, model...  17.3 us
    all_to_all x2, starting transfers between devices, routed_path(): lax.all_to_all(send_rows.reshape(local_experts, ep_size, cap_rows, model_...  10.2 us
    all_to_all x2, starting transfers between devices, routed_path(): lax.all_to_all(expert_out.reshape(local_experts, ep_size, cap_rows, model...  10.1 us
  transfers between devices with their start and end apart: 6, of which 4 were waited for; matrix products, arithmetic and copies ran while one was open for 57% of the time, Pallas kernels for 0%

commit v1 on v0

v1 whole, which is shorter than its diff:
```python
import functools

import jax
import jax.numpy as jnp
from jax import lax
from jax.experimental import pallas as pl
from jax.experimental.pallas import tpu as pltpu
from jax.sharding import PartitionSpec as P

MESH = pl.DeviceIdType.MESH
F32, BF16 = jnp.float32, jnp.bfloat16

TOK = 128
DIM = 1536
FF = 512
TOPK = 6
CAP = 24
NE = 16
PAIR = 2 * CAP
ROWS = 2 * PAIR
ALLR = NE * PAIR
CH = 512
NCH = DIM // CH
NRING = 3
W2G = 4
BF16_MAX = 3.3895313892515355e38


def dot(a, b):
    return jnp.dot(a, b, preferred_element_type=F32)


def kernel(tok_a, tok_b, e_a, s_a, e_b, s_b, g_a, g_b, sw1, sw3, sw2, rw1, rw3, rw2,
           out_a, out_b,
           ring, w2r, sw13, sw2v, tok, ytok, rowbuf, hid, rbuf, pmat, g3,
           sendr, sendl, recvr, recvl, xs, xr, acc, hso, hyo, hsi, ost, mi, mg,
           loc_sem, ring_sem, w2_sem, snd, rcv, credit):
    tp = lax.axis_index('tp')
    ep = lax.axis_index('ep')
    core = lax.rem(ep, 2)
    first = ep * NE
    dev_d = {'ep': ep + 1 - 2 * core}
    dev_x = {'ep': lax.rem(ep + 2, 4)}
    dev_y = {'tp': 1 - tp}
    toks, ids, gates = (tok_a, tok_b), (e_a, s_a, e_b, s_b), (g_a, g_b)
    outs = (out_a, out_b)

    def remote(src, dst, sem, dev):
        return pltpu.make_async_remote_copy(src_ref=src, dst_ref=dst, send_sem=snd.at[sem], recv_sem=rcv.at[sem],
                                            device_id=dev, device_id_type=MESH)

    own = [pltpu.make_async_copy(toks[m], tok.at[2 * m, pl.ds(0, TOK)], loc_sem.at[m]) for m in range(2)]
    own += [pltpu.make_async_copy(ids[i], mi.at[0, i], loc_sem.at[2 + i]) for i in range(4)]
    own += [pltpu.make_async_copy(gates[m], mg.at[0, m], loc_sem.at[6 + m]) for m in range(2)]
    shared = [pltpu.make_async_copy(sw1, sw13.at[0], loc_sem.at[8]),
              pltpu.make_async_copy(sw3, sw13.at[1], loc_sem.at[9]),
              pltpu.make_async_copy(sw2, sw2v.at[0], loc_sem.at[10])]

    def ring_copies(expert, slot):
        return (pltpu.make_async_copy(rw1.at[expert], ring.at[slot, 0], ring_sem.at[slot, 0]),
                pltpu.make_async_copy(rw3.at[expert], ring.at[slot, 1], ring_sem.at[slot, 1]))

    def w2_copy(i):
        return pltpu.make_async_copy(rw2.at[pl.ds(i * W2G, W2G)], w2r.at[pl.ds(i * W2G, W2G)], w2_sem.at[i])

    for c in own:
        c.start()
    shared[0].start()
    shared[1].start()
    for q in range(NRING):
        for c in ring_copies(q, q):
            c.start()
    for i in range(NE // W2G):
        w2_copy(i).start()
    shared[2].start()

    barrier = pltpu.get_barrier_semaphore()
    for dev in (dev_d, dev_x, dev_y):
        pl.semaphore_signal(barrier, inc=1, device_id=dev, device_id_type=MESH)
    pl.semaphore_wait(barrier, 3)

    d_meta = [remote(ids[i], mi.at[1, i], i, dev_d) for i in range(4)]
    d_meta += [remote(gates[m], mg.at[1, m], 4 + m, dev_d) for m in range(2)]
    x_meta = [remote(ids[i], mi.at[2, i], 6 + i, dev_x) for i in range(4)]
    x_meta += [remote(gates[m], mg.at[2, m], 10 + m, dev_x) for m in range(2)]
    f_meta = [remote(mi.at[2], mi.at[3], 12, dev_d), remote(mg.at[2], mg.at[3], 13, dev_d)]
    x_tok = [remote(toks[m], tok.at[2 * m + 1, pl.ds(0, TOK)], 14 + m, dev_x) for m in range(2)]
    d_tok = [remote(toks[m], tok.at[2 * m, pl.ds(TOK, TOK)], 16 + m, dev_d) for m in range(2)]
    f_tok = [remote(tok.at[2 * m + 1, pl.ds(0, TOK)], tok.at[2 * m + 1, pl.ds(TOK, TOK)], 18 + m, dev_d)
             for m in range(2)]
    y_tok = [remote(toks[m], ytok.at[pl.ds(m * TOK, TOK)], 20 + m, dev_y) for m in range(2)]
    half = pl.ds(pl.multiple_of(core * (FF // 2), FF // 2), FF // 2)
    y_w2 = remote(sw2.at[half], sw2v.at[1, half], 22, dev_y)
    f_w2 = remote(sw2v.at[1, half], sw2v.at[1, half], 23, dev_d)
    y_hid = remote(hyo, hsi, 24, dev_y)

    def d_rem(c):
        return remote(sendr.at[c], recvr.at[c], 25 + c, dev_d)

    def d_loc(c):
        return remote(sendl.at[c], recvl.at[c], 25 + NCH + c, dev_d)

    def x_part(m, c):
        return remote(xs.at[c], xr.at[m * NCH + c], 25 + 2 * NCH + m * NCH + c, dev_x)

    for c in x_meta + x_tok[:1] + d_meta + d_tok + x_tok[1:] + y_tok + [y_w2]:
        c.start()

    def swiglu(rows, w1, w3):
        p1 = dot(rows, w1)
        p3 = dot(rows, w3)
        return (jax.nn.silu(p1) * p3).astype(BF16)

    def build(m, pair):
        for pos in range(2):
            src = 2 * pair + pos
            slot = mi[src, 2 * m + 1]
            el = mi[src, 2 * m] - first
            ok = (slot >= 0) & (el >= 0) & (el < NE)
            rid = jnp.where(ok, el * PAIR + pos * CAP + slot, -1)
            g = mg[src, m]

            def block(b, _, pos=pos, rid=rid, g=g):
                at = pl.ds(pl.multiple_of(b * 128, 128), 128)
                row = lax.broadcasted_iota(jnp.int32, (128, TOK), 0) + b * 128
                hit = jnp.zeros((128, TOK), F32)
                gt = jnp.zeros((128, TOK), F32)
                for j in range(TOPK):
                    same = row == rid[j:j + 1, :]
                    hit = jnp.where(same, 1.0, hit)
                    gt = jnp.where(same, g[j:j + 1, :], gt)
                pmat[at, pos * TOK:(pos + 1) * TOK] = hit.astype(BF16)
                gg = gt.T
                hi = jnp.minimum(gg, BF16_MAX).astype(BF16)
                r1 = gg - hi.astype(F32)
                mid = r1.astype(BF16)
                lo = (r1 - mid.astype(F32)).astype(BF16)
                for k, v in enumerate((hi, mid, lo)):
                    g3[pair, k, pos * TOK:(pos + 1) * TOK, at] = v
                return 0
            lax.fori_loop(0, ALLR // 128, block, 0)

    def dispatch(m, pair):
        def group(b, _):
            p = pmat[pl.ds(pl.multiple_of(b * 4 * PAIR, 4 * PAIR), 4 * PAIR), :]
            rows = dot(p, tok[2 * m + pair]).astype(BF16)
            for i in range(4):
                rowbuf[b * 4 + i, pair * PAIR:(pair + 1) * PAIR, :] = rows[i * PAIR:(i + 1) * PAIR]
            return 0
        lax.fori_loop(0, NE // 4, group, 0)

    def phase1(m):
        def step(e, _):
            it = m * NE + e
            q = lax.rem(it, NRING)
            for c in ring_copies(e, q):
                c.wait()
            hid[e] = swiglu(rowbuf[e], ring[q, 0], ring[q, 1])

            @pl.when(it + NRING < 2 * NE)
            def _():
                for c in ring_copies(lax.rem(it + NRING, NE), q):
                    c.start()
            return 0
        lax.fori_loop(0, NE, step, 0)

    def combine(pair):
        r = rbuf[pair]
        return dot(g3[pair, 0], r) + dot(g3[pair, 1], r) + dot(g3[pair, 2], r)

    def phase2(m):
        def chunk(c, _):
            cols = pl.ds(pl.multiple_of(c * CH, CH), CH)

            def step(e, _):
                r = dot(hid[e], w2r[e, :, cols]).astype(BF16)
                at = pl.ds(pl.multiple_of(e * PAIR, PAIR), PAIR)
                rbuf[0, at, :] = r[:PAIR]
                rbuf[1, at, :] = r[PAIR:]
                return 0
            lax.fori_loop(0, NE, step, 0)
            if m == 1:
                d_rem(c).wait_send()
                d_loc(c).wait_send()
                x_part(0, c).wait_send()
            part = combine(1)
            sendr[c] = part[TOK:]
            d_rem(c).start()
            xs[c] = part[:TOK]
            part = combine(0)
            sendl[c] = part[TOK:]
            d_loc(c).start()
            acc[m * NCH + c] = part[:TOK]
            d_rem(c).wait_recv()
            xs[c] = xs[c] + recvr[c]
            x_part(m, c).start()
            return 0
        lax.fori_loop(0, NCH, chunk, 0)

    def take_local(m):
        def chunk(c, _):
            d_loc(c).wait_recv()
            acc[m * NCH + c] = acc[m * NCH + c] + recvl[c]
            return 0
        lax.fori_loop(0, NCH, chunk, 0)

    for c in own:
        c.wait()
    shared[0].wait()
    shared[1].wait()
    for m in range(2):
        hso[m] = swiglu(tok[2 * m, :TOK], sw13[0], sw13[1])
    for c in d_meta + d_tok:
        c.wait_recv()
    build(0, 0)
    dispatch(0, 0)
    for c in x_meta:
        c.wait_recv()
    for c in f_meta:
        c.start()
    for c in f_meta:
        c.wait_recv()
    build(0, 1)
    x_tok[0].wait_recv()
    f_tok[0].start()
    f_tok[0].wait_recv()
    dispatch(0, 1)

    phase1(0)
    x_tok[1].wait_recv()
    f_tok[1].start()
    for i in range(NE // W2G):
        w2_copy(i).wait()
    phase2(0)
    for c in y_tok:
        c.wait_recv()
    hyo[0] = swiglu(ytok[:TOK], sw13[0], sw13[1])
    hyo[1] = swiglu(ytok[TOK:], sw13[0], sw13[1])
    y_hid.start()
    take_local(0)
    pl.semaphore_signal(credit, inc=1, device_id=dev_d, device_id_type=MESH)

    build(1, 0)
    dispatch(1, 0)
    build(1, 1)
    f_tok[1].wait_recv()
    dispatch(1, 1)
    phase1(1)
    y_w2.wait_recv()
    f_w2.start()
    pl.semaphore_wait(credit, 1)
    phase2(1)
    take_local(1)

    shared[2].wait()
    f_w2.wait_recv()
    y_hid.wait_recv()
    for m in range(2):
        def base(c, _, m=m):
            cols = pl.ds(pl.multiple_of(c * CH, CH), CH)
            s = dot(hso[m], sw2v[0, :, cols]) + dot(hsi[m], sw2v[1, :, cols])
            acc[m * NCH + c] = acc[m * NCH + c] + s + tok[2 * m, pl.ds(0, TOK), cols].astype(F32)
            return 0
        lax.fori_loop(0, NCH, base, 0)
    put = [pltpu.make_async_copy(ost.at[m], outs[m], loc_sem.at[11 + m]) for m in range(2)]
    for m in range(2):
        def last(c, _, m=m):
            cols = pl.ds(pl.multiple_of(c * CH, CH), CH)
            x_part(m, c).wait_recv()
            ost[m, :, cols] = (acc[m * NCH + c] + xr[m * NCH + c]).astype(BF16)
            return 0
        lax.fori_loop(0, NCH, last, 0)
        put[m].start()

    for c in x_meta + x_tok + d_meta + d_tok + f_meta + f_tok + y_tok + [y_w2, f_w2, y_hid]:
        c.wait_send()
    for c in range(NCH):
        d_rem(c).wait_send()
        d_loc(c).wait_send()
        x_part(1, c).wait_send()
    for c in put:
        c.wait()


def solution(mesh):
    tok_spec = P(('data', 'ep', 'tp'), None)
    in_specs = (tok_spec,) * 8 + (P(None, 'tp'), P(None, 'tp'), P('tp', None), P('ep', None, None), P('ep', None, None), P('ep', None, None))
    nsem = 25 + 4 * NCH
    scratch = [
        pltpu.VMEM((NRING, 2, DIM, FF), BF16),
        pltpu.VMEM((NE, FF, DIM), BF16),
        pltpu.VMEM((2, DIM, FF), BF16),
        pltpu.VMEM((2, FF, DIM), BF16),
        pltpu.VMEM((4, 2 * TOK, DIM), BF16),
        pltpu.VMEM((2 * TOK, DIM), BF16),
        pltpu.VMEM((NE, ROWS, DIM), BF16),
        pltpu.VMEM((NE, ROWS, FF), BF16),
        pltpu.VMEM((2, ALLR, CH), BF16),
        pltpu.VMEM((ALLR, 2 * TOK), BF16),
        pltpu.VMEM((2, 3, 2 * TOK, ALLR), BF16),
        pltpu.VMEM((NCH, TOK, CH), F32),
        pltpu.VMEM((NCH, TOK, CH), F32),
        pltpu.VMEM((NCH, TOK, CH), F32),
        pltpu.VMEM((NCH, TOK, CH), F32),
        pltpu.VMEM((NCH, TOK, CH), F32),
        pltpu.VMEM((2 * NCH, TOK, CH), F32),
        pltpu.VMEM((2 * NCH, TOK, CH), F32),
        pltpu.VMEM((2, TOK, FF), BF16),
        pltpu.VMEM((2, TOK, FF), BF16),
        pltpu.VMEM((2, TOK, FF), BF16),
        pltpu.VMEM((2, TOK, DIM), BF16),
        pltpu.VMEM((4, 4, TOPK, TOK), jnp.int32),
        pltpu.VMEM((4, 2, TOPK, TOK), F32),
        pltpu.SemaphoreType.DMA((13,)),
        pltpu.SemaphoreType.DMA((NRING, 2)),
        pltpu.SemaphoreType.DMA((NE // W2G,)),
        pltpu.SemaphoreType.DMA((nsem,)),
        pltpu.SemaphoreType.DMA((nsem,)),
        pltpu.SemaphoreType.REGULAR,
    ]

    def layer_local(tokens_a, tokens_b, experts_a, experts_b, gates_a, gates_b, slots_a, slots_b, shared_w1, shared_w3, shared_w2, routed_w1, routed_w3, routed_w2):
        return pl.pallas_call(
            kernel,
            out_shape=(jax.ShapeDtypeStruct((TOK, DIM), BF16),) * 2,
            in_specs=[pl.BlockSpec(memory_space=pl.ANY)] * 14,
            out_specs=(pl.BlockSpec(memory_space=pl.ANY),) * 2,
            scratch_shapes=scratch,
            compiler_params=pltpu.CompilerParams(collective_id=0, has_side_effects=True, vmem_limit_bytes=67043328),
        )(tokens_a, tokens_b, experts_a.T, slots_a.T, experts_b.T, slots_b.T, gates_a.T, gates_b.T,
          shared_w1, shared_w3, shared_w2, routed_w1, routed_w3, routed_w2)

    return jax.shard_map(layer_local, mesh=mesh, in_specs=in_specs, out_specs=(tok_spec, tok_spec), check_vma=False)
```

time: 289 us -> 104 us (0.36)
  Pallas kernels: 0 us -> 99.4 us
  matrix products: 97.1 us -> 0 us
  local copies, waits for them, and re-layouts: 65.4 us -> 3.53 us
  waiting for transfers between devices: 48.1 us -> 0 us
  blocking collectives: 26.4 us -> 0 us
  starting transfers between devices: 20.4 us -> 0 us
  other arithmetic: 16.5 us -> 0 us
  between operations: 14.3 us -> 0.64 us
    pallas_call x0 -> x1, Pallas kernels: none -> 99.4 us  [layer_local(): pl.pallas_call(kernel, out_shape=(jax.ShapeDtypeStruct((TOK, DIM), BF16),...]
    dot_general x10 -> x0, matrix products: 97.1 us -> none  [the longest x2 53.4 us: routed_path(): jnp.einsum('erf,efd->erd', hidden, routed_w2, preferred_element_type=jnp....]
    all_to_all x4 -> x0, waiting for transfers between devices: 48 us -> none  [the longest x2 30.7 us: routed_path(): lax.all_to_all(send_rows.reshape(local_experts, ep_size, cap_rows, model_...]
    gather x4 -> x0, local copies, waits for them, and re-layouts: 27.5 us -> none  [routed_path(): jnp.take(back_rows.reshape(num_rows, model_dim), jnp.maximum(row_ids, 0),...]
    all_gather x2 -> x0, blocking collectives: 26.4 us -> none  [shared_path(): gathered = lax.all_gather(x_local, 'tp', axis=0, tiled=True)]
    all_to_all x4 -> x0, starting transfers between devices: 20.4 us -> none  [the longest x2 10.2 us: routed_path(): lax.all_to_all(send_rows.reshape(local_experts, ep_size, cap_rows, model_...]
    all_to_all x4 -> x0, local copies, waits for them, and re-layouts: 15.7 us -> none  [the longest x2 10 us: routed_path(): lax.all_to_all(expert_out.reshape(local_experts, ep_size, cap_rows, model...]
    reshape x4 -> x0, local copies, waits for them, and re-layouts: 15 us -> none  [the longest x2 9.95 us: routed_path(): expert_out.reshape(local_experts, ep_size, cap_rows, model_dim)]
  transfers between devices with their start and end apart: 6 -> 0, of which waited for: 4 -> 0; matrix products, arithmetic and copies ran while one was open for 57% -> 0% of each run, Pallas kernels for 0% -> 0%
where the time goes in v1:
time: 104 us
  Pallas kernels  99.4 us (96%)
  local copies, waits for them, and re-layouts  3.53 us (3%)
    pallas_call x1, Pallas kernels, layer_local(): pl.pallas_call(kernel, out_shape=(jax.ShapeDtypeStruct((TOK, DIM), BF16),...  99.4 us
    unnamed x2, local copies, waits for them, and re-layouts  3.53 us

profile of v1, /device:TPU:0, one launch (start us, length us, event | category | flops | bytes accessed | tf_op | source)
XLA Modules:
  0.0 103.5 jit_solution(13737662475208195757)
XLA Ops:
  0.6 99.4 %shard_map.149 = (bf16[128,1536]{1,0:T(8,128)(2,1)}, bf16[128,1536]{1,0:T(8,128)(2,1)}) custom-call(bf16[128,1536]{1,0:T(8,128)(2,1)} %tok_a.1, bf16[128,1536]{1,0:T(8,128)(2,1)} %tok_b.1, s32[6,128]{1,0:T(8,128)} %bitcast.6, s32[6,128]{1,0:T(8,128)} %bitcast.7, s32[6,128]{1,0:T(8,128)} %bitcast.8, s32[6,128]{1,0:T(8,128)} %bitcast.9, f32[6,128]{1,0:T(8,128)} %bitcast.10, ...), custom_call_target="tpu_custom_call" | custom-call | tf_op jit(solution)/shard_map/pallas_call | solution.py:323
  100.0 1.8 %copy.18 = bf16[128,1536]{1,0:T(8,128)(2,1)} copy(bf16[128,1536]{1,0:T(8,128)(2,1)} %get-tuple-element.4) | data formatting | bytes 786432
  101.8 1.8 %copy.19 = bf16[128,1536]{1,0:T(8,128)(2,1)} copy(bf16[128,1536]{1,0:T(8,128)(2,1)} %get-tuple-element.5) | data formatting | bytes 786432

commit v2 on v0

v2 whole, which is shorter than its diff:
```python
import functools

import jax
import jax.numpy as jnp
from jax import lax
from jax.experimental import pallas as pl
from jax.experimental.pallas import tpu as pltpu
from jax.sharding import PartitionSpec as P

MESH = pl.DeviceIdType.MESH
F32, BF16 = jnp.float32, jnp.bfloat16

TOK = 128
DIM = 1536
FF = 512
TOPK = 6
CAP = 24
NE = 16
SRC = 8
ROWS = SRC * CAP
SROWS = NE * CAP
KC = 512
NK = DIM // KC
CH = 512
NCH = DIM // CH
NS = 24
N1 = NK * NE
N2 = NCH * NE // 2
BF16_MAX = 3.3895313892515355e38


def dot(a, b):
    return jnp.dot(a, b, preferred_element_type=F32)


def kernel(tok_a, tok_b, e_a, s_a, e_b, s_b, g_a, g_b, sw1, sw3, sw2, rw1, rw3, rw2,
           out_a, out_b,
           ring, sw13, sw2v, tok, ytok, buf, pf, hid, pmat, g3,
           recvr, recvl, xr, hso, hyo, hsi, ost, mi, mg,
           loc_sem, ring_sem, snd, rcv):
    tp = lax.axis_index('tp')
    ep = lax.axis_index('ep')
    core = lax.rem(ep, 2)
    first = ep * NE
    dev_d = {'ep': ep + 1 - 2 * core}
    dev_x = {'ep': lax.rem(ep + 2, 4)}
    dev_y = {'tp': 1 - tp}
    toks, ids, gates = (tok_a, tok_b), (e_a, s_a, e_b, s_b), (g_a, g_b)
    outs = (out_a, out_b)

    def local(src, dst, sem):
        return pltpu.make_async_copy(src, dst, loc_sem.at[sem])

    def remote(src, dst, sem, dev):
        return pltpu.make_async_remote_copy(src_ref=src, dst_ref=dst, send_sem=snd.at[sem], recv_sem=rcv.at[sem],
                                            device_id=dev, device_id_type=MESH)

    def mult(i, k):
        return i * k if isinstance(i, int) else pl.multiple_of(i * k, k)

    def part(i, k):
        return pl.ds(mult(i, k), k)

    own_meta = [local(ids[i], mi.at[0, i], i) for i in range(4)] + [local(gates[m], mg.at[0, m], 4 + m) for m in range(2)]
    own_tok = [local(toks[m], tok.at[2 * m, pl.ds(0, TOK)], 6 + m) for m in range(2)]
    shared = [local(sw1, sw13.at[0], 8), local(sw3, sw13.at[1], 9), local(sw2, sw2v.at[0], 10)]

    def put(m, c):
        cols = part(c, CH)
        return local(ost.at[m, :, cols], outs[m].at[:, cols], 11 + m * NCH + c)

    def first_item(n, slot):
        e, rows = n % NE, part(n // NE, KC)
        return (pltpu.make_async_copy(rw1.at[e, rows], ring.at[slot, pl.ds(0, KC)], ring_sem.at[slot, 0]),
                pltpu.make_async_copy(rw3.at[e, rows], ring.at[slot, pl.ds(KC, KC)], ring_sem.at[slot, 1]))

    def second_item(n, slot):
        g, cols = n % (NE // 2), part(n // (NE // 2), CH)
        return (pltpu.make_async_copy(rw2.at[2 * g, :, cols], ring.at[slot, pl.ds(0, FF)], ring_sem.at[slot, 0]),
                pltpu.make_async_copy(rw2.at[2 * g + 1, :, cols], ring.at[slot, pl.ds(FF, FF)], ring_sem.at[slot, 1]))

    def refill(n):
        slot = n % NS

        @pl.when(n < N1)
        def _():
            for c in first_item(n, slot):
                c.start()

        @pl.when((n >= N1) & (n < N1 + N2))
        def _():
            for c in second_item(n - N1, slot):
                c.start()

    d_meta = [remote(ids[i], mi.at[1, i], i, dev_d) for i in range(4)]
    d_meta += [remote(gates[m], mg.at[1, m], 4 + m, dev_d) for m in range(2)]
    x_meta = [remote(ids[i], mi.at[2, i], 6 + i, dev_x) for i in range(4)]
    x_meta += [remote(gates[m], mg.at[2, m], 10 + m, dev_x) for m in range(2)]
    f_meta = [remote(mi.at[2], mi.at[3], 12, dev_d), remote(mg.at[2], mg.at[3], 13, dev_d)]
    d_tok = [remote(toks[m], tok.at[2 * m, pl.ds(TOK, TOK)], 14 + m, dev_d) for m in range(2)]
    y_tok = [remote(toks[m], ytok.at[pl.ds(m * TOK, TOK)], 16 + m, dev_y) for m in range(2)]
    half = part(core, FF // 2)
    y_w2 = remote(sw2.at[half], sw2v.at[1, half], 18, dev_y)
    f_w2 = remote(sw2v.at[1, half], sw2v.at[1, half], 19, dev_d)
    y_hid = remote(hyo, hsi, 20, dev_y)
    x_tok, f_tok = [], []
    for k in range(NK):
        cols = part(k, KC)
        x_tok.append([remote(toks[m].at[:, cols], tok.at[2 * m + 1, pl.ds(0, TOK), cols], 21 + 2 * k + m, dev_x)
                      for m in range(2)])
        f_tok.append([remote(tok.at[2 * m + 1, pl.ds(0, TOK), cols], tok.at[2 * m + 1, pl.ds(TOK, TOK), cols],
                             21 + 2 * NK + 2 * k + m, dev_d) for m in range(2)])
    base_sem = 21 + 4 * NK

    def send_r(i):
        return part(i, TOK)

    def send_l(i):
        return part(2 * NCH + i, TOK)

    def send_x(i):
        return part(4 * NCH + i, TOK)

    def kept(i):
        return part(6 * NCH + i, TOK)

    def d_rem(i):
        return remote(pf.at[send_r(i)], recvr.at[i], base_sem + i, dev_d)

    def d_loc(i):
        return remote(pf.at[send_l(i)], recvl.at[i], base_sem + 2 * NCH + i, dev_d)

    def x_part(i):
        return remote(pf.at[send_x(i)], xr.at[i], base_sem + 4 * NCH + i, dev_x)

    def swiglu(rows, w1, w3):
        p1 = dot(rows, w1)
        p3 = dot(rows, w3)
        return (jax.nn.silu(p1) * p3).astype(BF16)

    def build(src):
        def block(i, _):
            m, b = i // (SROWS // 128), i % (SROWS // 128)
            at = part(b, 128)
            slot = mi[src, 2 * m + 1]
            el = mi[src, 2 * m] - first
            ok = (slot >= 0) & (el >= 0) & (el < NE)
            rid = jnp.where(ok, el * CAP + slot, -1) - b * 128
            g = mg[src, m]
            row = lax.broadcasted_iota(jnp.int32, (128, TOK), 0)
            hit = jnp.zeros((128, TOK), F32)
            gt = jnp.zeros((128, TOK), F32)
            for j in range(TOPK):
                same = row == rid[j:j + 1, :]
                hit = jnp.where(same, 1.0, hit)
                gt = jnp.where(same, g[j:j + 1, :], gt)
            pmat[4 * m + src, at, :] = hit.astype(BF16)
            gg = gt.T
            hi = jnp.minimum(gg, BF16_MAX).astype(BF16)
            r1 = gg - hi.astype(F32)
            mid = r1.astype(BF16)
            lo = (r1 - mid.astype(F32)).astype(BF16)
            for k, v in enumerate((hi, mid, lo)):
                g3[4 * m + src, k * TOK:(k + 1) * TOK, at] = v
            return 0
        lax.fori_loop(0, 2 * SROWS // 128, block, 0)

    def dispatch(k, pair):
        def group(i, _):
            m, cols = i // (KC // 256), pl.ds(pl.multiple_of(k * KC + (i % (KC // 256)) * 256, 256), 256)
            to = part(i % (KC // 256), 256)
            s = 4 * m + 2 * pair
            r0 = dot(pmat[s], tok[2 * m + pair, pl.ds(0, TOK), cols])
            r1 = dot(pmat[s + 1], tok[2 * m + pair, pl.ds(TOK, TOK), cols])
            for e in range(NE):
                both = jnp.concatenate([r0[e * CAP:(e + 1) * CAP], r1[e * CAP:(e + 1) * CAP]], axis=0)
                buf[pl.ds(pl.multiple_of(e * ROWS + s * CAP, 2 * CAP), 2 * CAP), to] = both.astype(BF16)
            return 0
        lax.fori_loop(0, 2 * (KC // 256), group, 0)

    def stage1(k):
        def step(i, _):
            for u in range(2):
                n = k * NE + 2 * i + u
                for c in first_item(n, n % NS):
                    c.wait()
            for u in range(2):
                e = 2 * i + u
                n = k * NE + e
                slot = n % NS
                rows = buf[part(e, ROWS), :]
                p1 = dot(rows, ring[slot, :KC])
                p3 = dot(rows, ring[slot, KC:])
                at1, at3 = part(2 * e, ROWS), part(2 * e + 1, ROWS)
                if k:
                    p1 = p1 + pf[at1, :]
                    p3 = p3 + pf[at3, :]
                if k < NK - 1:
                    pf[at1, :] = p1
                    pf[at3, :] = p3
                else:
                    hid[e] = (jax.nn.silu(p1) * p3).astype(BF16)
            for u in range(2):
                refill(k * NE + 2 * i + u + NS)
            return 0
        lax.fori_loop(0, NE // 2, step, 0)

    def combine(s):
        q = dot(g3[s], buf[part(s, SROWS), :])
        return q[:TOK] + q[TOK:2 * TOK] + q[2 * TOK:]

    def stage2(c):
        def step(g, _):
            n = c * (NE // 2) + g
            slot = (N1 + n) % NS
            for d in second_item(n, slot):
                d.wait()
            r0 = dot(hid[2 * g], ring[slot, :FF])
            r1 = dot(hid[2 * g + 1], ring[slot, FF:])
            for s in range(SRC):
                both = jnp.concatenate([r0[s * CAP:(s + 1) * CAP], r1[s * CAP:(s + 1) * CAP]], axis=0)
                buf[pl.ds(pl.multiple_of(s * SROWS + g * 2 * CAP, 2 * CAP), 2 * CAP), :] = both.astype(BF16)
            refill(N1 + n + NS)
            return 0
        lax.fori_loop(0, NE // 2, step, 0)

        def to_die(m, _):
            pf[send_r(m * NCH + c), :] = combine(4 * m + 3)
            d_rem(m * NCH + c).start()
            return 0
        lax.fori_loop(0, 2, to_die, 0)

        def mine(m, _):
            pf[send_x(m * NCH + c), :] = combine(4 * m + 2)
            return 0
        lax.fori_loop(0, 2, mine, 0)

        def to_x(m, _):
            i = m * NCH + c
            d_rem(i).wait_recv()
            pf[send_x(i), :] = pf[send_x(i), :] + recvr[i]
            x_part(i).start()
            return 0
        lax.fori_loop(0, 2, to_x, 0)

        def home(m, _):
            i = m * NCH + c
            pf[send_l(i), :] = combine(4 * m + 1)
            d_loc(i).start()
            pf[kept(i), :] = combine(4 * m)
            return 0
        lax.fori_loop(0, 2, home, 0)

    for c in own_meta + own_tok:
        c.start()
    barrier = pltpu.get_barrier_semaphore()
    for dev in (dev_d, dev_x, dev_y):
        pl.semaphore_signal(barrier, inc=1, device_id=dev, device_id_type=MESH)
    pl.semaphore_wait(barrier, 3)
    for c in x_meta + d_meta + x_tok[0] + d_tok + x_tok[1] + x_tok[2] + y_tok + [y_w2]:
        c.start()
    for c in own_meta + own_tok:
        c.wait()
    for c in shared[:2]:
        c.start()

    def fill(n, _):
        for c in first_item(n, n):
            c.start()
        return 0
    lax.fori_loop(0, NS, fill, 0)
    shared[2].start()

    build(0)
    for c in d_meta + x_meta:
        c.wait_recv()
    for c in f_meta:
        c.start()
    build(1)
    build(2)
    for c in f_meta + d_tok:
        c.wait_recv()
    build(3)
    for c in shared[:2]:
        c.wait()
    for m in range(2):
        hso[m] = swiglu(tok[2 * m, :TOK], sw13[0], sw13[1])

    for k in range(NK):
        for c in x_tok[k]:
            c.wait_recv()
        for c in f_tok[k]:
            c.start()
        dispatch(k, 0)
        for c in f_tok[k]:
            c.wait_recv()
        dispatch(k, 1)
        stage1(k)

    stage2(0)
    for c in y_tok:
        c.wait_recv()
    for m in range(2):
        hyo[m] = swiglu(ytok[m * TOK:(m + 1) * TOK], sw13[0], sw13[1])
    y_hid.start()
    for c in range(1, NCH):
        stage2(c)
    y_w2.wait_recv()
    f_w2.start()
    shared[2].wait()
    f_w2.wait_recv()
    y_hid.wait_recv()

    for m in range(2):
        def base(c, _, m=m):
            cols, i = part(c, CH), m * NCH + c
            d_loc(i).wait_recv()
            s = dot(hso[m], sw2v[0, :, cols]) + dot(hsi[m], sw2v[1, :, cols])
            pf[kept(i), :] = pf[kept(i), :] + recvl[i] + s + tok[2 * m, pl.ds(0, TOK), cols].astype(F32)
            return 0
        lax.fori_loop(0, NCH, base, 0)

    for c in range(NCH):
        for m in range(2):
            i = m * NCH + c
            x_part(i).wait_recv()
            ost[m, :, c * CH:(c + 1) * CH] = (pf[kept(i), :] + xr[i]).astype(BF16)
            put(m, c).start()

    for c in x_meta + d_meta + f_meta + d_tok + y_tok + [y_w2, f_w2, y_hid] + sum(x_tok, []) + sum(f_tok, []):
        c.wait_send()
    for i in range(2 * NCH):
        d_rem(i).wait_send()
        d_loc(i).wait_send()
        x_part(i).wait_send()
    for m in range(2):
        for c in range(NCH):
            put(m, c).wait()


def solution(mesh):
    tok_spec = P(('data', 'ep', 'tp'), None)
    in_specs = (tok_spec,) * 8 + (P(None, 'tp'), P(None, 'tp'), P('tp', None), P('ep', None, None), P('ep', None, None), P('ep', None, None))
    nsem = 21 + 4 * NK + 6 * NCH
    scratch = [
        pltpu.VMEM((NS, 2 * KC, FF), BF16),
        pltpu.VMEM((2, DIM, FF), BF16),
        pltpu.VMEM((2, FF, DIM), BF16),
        pltpu.VMEM((4, 2 * TOK, DIM), BF16),
        pltpu.VMEM((2 * TOK, DIM), BF16),
        pltpu.VMEM((NE * ROWS, KC), BF16),
        pltpu.VMEM((2 * NE * ROWS, FF), F32),
        pltpu.VMEM((NE, ROWS, FF), BF16),
        pltpu.VMEM((SRC, SROWS, TOK), BF16),
        pltpu.VMEM((SRC, 3 * TOK, SROWS), BF16),
        pltpu.VMEM((2 * NCH, TOK, CH), F32),
        pltpu.VMEM((2 * NCH, TOK, CH), F32),
        pltpu.VMEM((2 * NCH, TOK, CH), F32),
        pltpu.VMEM((2, TOK, FF), BF16),
        pltpu.VMEM((2, TOK, FF), BF16),
        pltpu.VMEM((2, TOK, FF), BF16),
        pltpu.VMEM((2, TOK, DIM), BF16),
        pltpu.VMEM((4, 4, TOPK, TOK), jnp.int32),
        pltpu.VMEM((4, 2, TOPK, TOK), F32),
        pltpu.SemaphoreType.DMA((11 + 2 * NCH,)),
        pltpu.SemaphoreType.DMA((NS, 2)),
        pltpu.SemaphoreType.DMA((nsem,)),
        pltpu.SemaphoreType.DMA((nsem,)),
    ]

    def layer_local(tokens_a, tokens_b, experts_a, experts_b, gates_a, gates_b, slots_a, slots_b, shared_w1, shared_w3, shared_w2, routed_w1, routed_w3, routed_w2):
        return pl.pallas_call(
            kernel,
            out_shape=(jax.ShapeDtypeStruct((TOK, DIM), BF16),) * 2,
            in_specs=[pl.BlockSpec(memory_space=pl.ANY)] * 14,
            out_specs=(pl.BlockSpec(memory_space=pl.ANY),) * 2,
            scratch_shapes=scratch,
            compiler_params=pltpu.CompilerParams(collective_id=0, has_side_effects=True, vmem_limit_bytes=67043328),
        )(tokens_a, tokens_b, experts_a.T, slots_a.T, experts_b.T, slots_b.T, gates_a.T, gates_b.T,
          shared_w1, shared_w3, shared_w2, routed_w1, routed_w3, routed_w2)

    return jax.shard_map(layer_local, mesh=mesh, in_specs=in_specs, out_specs=(tok_spec, tok_spec), check_vma=False)
```

time: 289 us -> 80.3 us (0.28)
  matrix products: 97.1 us -> 0 us
  Pallas kernels: 0 us -> 75.9 us
  local copies, waits for them, and re-layouts: 65.4 us -> 3.53 us
  waiting for transfers between devices: 48.1 us -> 0 us
  blocking collectives: 26.4 us -> 0 us
  starting transfers between devices: 20.4 us -> 0 us
  other arithmetic: 16.5 us -> 0 us
  between operations: 14.3 us -> 0.64 us
    dot_general x10 -> x0, matrix products: 97.1 us -> none  [the longest x2 53.4 us: routed_path(): jnp.einsum('erf,efd->erd', hidden, routed_w2, preferred_element_type=jnp....]
    pallas_call x0 -> x1, Pallas kernels: none -> 75.9 us  [layer_local(): pl.pallas_call(kernel, out_shape=(jax.ShapeDtypeStruct((TOK, DIM), BF16),...]
    all_to_all x4 -> x0, waiting for transfers between devices: 48 us -> none  [the longest x2 30.7 us: routed_path(): lax.all_to_all(send_rows.reshape(local_experts, ep_size, cap_rows, model_...]
    gather x4 -> x0, local copies, waits for them, and re-layouts: 27.5 us -> none  [routed_path(): jnp.take(back_rows.reshape(num_rows, model_dim), jnp.maximum(row_ids, 0),...]
    all_gather x2 -> x0, blocking collectives: 26.4 us -> none  [shared_path(): gathered = lax.all_gather(x_local, 'tp', axis=0, tiled=True)]
    all_to_all x4 -> x0, starting transfers between devices: 20.4 us -> none  [the longest x2 10.2 us: routed_path(): lax.all_to_all(send_rows.reshape(local_experts, ep_size, cap_rows, model_...]
    all_to_all x4 -> x0, local copies, waits for them, and re-layouts: 15.7 us -> none  [the longest x2 10 us: routed_path(): lax.all_to_all(expert_out.reshape(local_experts, ep_size, cap_rows, model...]
    reshape x4 -> x0, local copies, waits for them, and re-layouts: 15 us -> none  [the longest x2 9.95 us: routed_path(): expert_out.reshape(local_experts, ep_size, cap_rows, model_dim)]
  transfers between devices with their start and end apart: 6 -> 0, of which waited for: 4 -> 0; matrix products, arithmetic and copies ran while one was open for 57% -> 0% of each run, Pallas kernels for 0% -> 0%
where the time goes in v2:
time: 80.3 us; the launch traced here: 80.1 us
  Pallas kernels  75.9 us (95%)
  local copies, waits for them, and re-layouts  3.53 us (4%)
    pallas_call x1, Pallas kernels, layer_local(): pl.pallas_call(kernel, out_shape=(jax.ShapeDtypeStruct((TOK, DIM), BF16),...  75.9 us
    unnamed x2, local copies, waits for them, and re-layouts  3.53 us

profile of v2, /device:TPU:0, one launch (start us, length us, event | category | flops | bytes accessed | tf_op | source)
XLA Modules:
  0.0 80.1 jit_solution(11977622387058807110)
XLA Ops:
  0.6 75.9 %shard_map.149 = (bf16[128,1536]{1,0:T(8,128)(2,1)}, bf16[128,1536]{1,0:T(8,128)(2,1)}) custom-call(bf16[128,1536]{1,0:T(8,128)(2,1)} %tok_a.1, bf16[128,1536]{1,0:T(8,128)(2,1)} %tok_b.1, s32[6,128]{1,0:T(8,128)} %bitcast.6, s32[6,128]{1,0:T(8,128)} %bitcast.7, s32[6,128]{1,0:T(8,128)} %bitcast.8, s32[6,128]{1,0:T(8,128)} %bitcast.9, f32[6,128]{1,0:T(8,128)} %bitcast.10, ...), custom_call_target="tpu_custom_call" | custom-call | tf_op jit(solution)/shard_map/pallas_call | solution.py:372
  76.6 1.8 %copy.18 = bf16[128,1536]{1,0:T(8,128)(2,1)} copy(bf16[128,1536]{1,0:T(8,128)(2,1)} %get-tuple-element.4) | data formatting | bytes 786432
  78.3 1.8 %copy.19 = bf16[128,1536]{1,0:T(8,128)(2,1)} copy(bf16[128,1536]{1,0:T(8,128)(2,1)} %get-tuple-element.5) | data formatting | bytes 786432

commit v3 on v2

v3 whole, which is shorter than its diff:
```python
import functools

import jax
import jax.numpy as jnp
from jax import lax
from jax.experimental import pallas as pl
from jax.experimental.pallas import tpu as pltpu
from jax.sharding import PartitionSpec as P

MESH = pl.DeviceIdType.MESH
F32, BF16 = jnp.float32, jnp.bfloat16

TOK = 128
DIM = 1536
FF = 512
TOPK = 6
CAP = 24
NE = 16
SRC = 8
ROWS = SRC * CAP
SROWS = NE * CAP
KC = 512
NK = DIM // KC
CHS = (256, 512, 512, 256)
NCH = len(CHS)
COL = [sum(CHS[:c]) for c in range(NCH)]
NS = 24
N1 = NK * NE
ITEM2 = [N1 + COL[c] // 64 for c in range(NCH)]
NITEM = N1 + DIM // 64
BF16_MAX = 3.3895313892515355e38


def dot(a, b):
    return jnp.dot(a, b, preferred_element_type=F32)


def kernel(tok_a, tok_b, e_a, s_a, e_b, s_b, g_a, g_b, sw1, sw3, sw2, rw1, rw3, rw2,
           out_ab,
           ring, sw13, sw2v, tok, ytok, buf, pf, hid, pmat, g3,
           recvr, recvl, xr, hso, hyo, hsi, ost, mi, mg,
           loc_sem, ring_sem, snd, rcv):
    tp = lax.axis_index('tp')
    ep = lax.axis_index('ep')
    core = lax.rem(ep, 2)
    first = ep * NE
    dev_d = {'ep': ep + 1 - 2 * core}
    dev_x = {'ep': lax.rem(ep + 2, 4)}
    dev_y = {'tp': 1 - tp}
    toks, ids, gates = (tok_a, tok_b), (e_a, s_a, e_b, s_b), (g_a, g_b)

    def local(src, dst, sem):
        return pltpu.make_async_copy(src, dst, loc_sem.at[sem])

    def remote(src, dst, sem, dev):
        return pltpu.make_async_remote_copy(src_ref=src, dst_ref=dst, send_sem=snd.at[sem], recv_sem=rcv.at[sem],
                                            device_id=dev, device_id_type=MESH)

    def mult(i, k):
        return i * k if isinstance(i, int) else pl.multiple_of(i * k, k)

    def part(i, k):
        return pl.ds(mult(i, k), k)

    own_meta = [local(ids[i], mi.at[0, i], i) for i in range(4)] + [local(gates[m], mg.at[0, m], 4 + m) for m in range(2)]
    own_tok = [local(toks[m], tok.at[0, m], 6 + m) for m in range(2)]
    shared = [local(sw1, sw13.at[0], 8), local(sw3, sw13.at[1], 9), local(sw2, sw2v.at[0], 10)]

    def out_cols(c):
        return pl.ds(COL[c], CHS[c])

    def put(m, c):
        return local(ost.at[m, :, out_cols(c)], out_ab.at[m, :, out_cols(c)], 11 + m * NCH + c)

    def first_item(n, slot):
        e, rows = n % NE, part(n // NE, KC)
        return (pltpu.make_async_copy(rw1.at[e, rows], ring.at[slot, pl.ds(0, KC)], ring_sem.at[slot, 0]),
                pltpu.make_async_copy(rw3.at[e, rows], ring.at[slot, pl.ds(KC, KC)], ring_sem.at[slot, 1]))

    def second_item(c, q, slot):
        w = CHS[c]
        per_row = FF // w
        res = []
        for i in range(2 * per_row):
            to = ring.at[slot, pl.ds((i // per_row) * FF, FF), pl.ds((i % per_row) * w, w)]
            res.append(pltpu.make_async_copy(rw2.at[2 * per_row * q + i, :, out_cols(c)], to, ring_sem.at[slot, i]))
        return res

    segments = [(0, N1, lambda n, slot: first_item(n, slot))]
    for c in range(NCH):
        stop = ITEM2[c + 1] if c + 1 < NCH else NITEM
        segments.append((ITEM2[c], stop, lambda n, slot, c=c: second_item(c, n - ITEM2[c], slot)))

    def refill(n, low, high):
        for a, b, copies in segments:
            if a >= high or b <= low:
                continue

            def go(copies=copies):
                for c in copies(n, n % NS):
                    c.start()
            if a <= low and high <= b:
                go()
            else:
                pl.when((n >= a) & (n < b))(go)

    d_meta = [remote(ids[i], mi.at[1, i], i, dev_d) for i in range(4)]
    d_meta += [remote(gates[m], mg.at[1, m], 4 + m, dev_d) for m in range(2)]
    x_meta = [remote(ids[i], mi.at[2, i], 6 + i, dev_x) for i in range(4)]
    x_meta += [remote(gates[m], mg.at[2, m], 10 + m, dev_x) for m in range(2)]
    f_meta = [remote(mi.at[2], mi.at[3], 12, dev_d), remote(mg.at[2], mg.at[3], 13, dev_d)]
    d_tok = [remote(toks[m], tok.at[1, m], 14 + m, dev_d) for m in range(2)]
    y_tok = [remote(toks[m], ytok.at[pl.ds(m * TOK, TOK)], 16 + m, dev_y) for m in range(2)]
    half = part(core, FF // 2)
    y_w2 = remote(sw2.at[half], sw2v.at[1, half], 18, dev_y)
    f_w2 = remote(sw2v.at[1, half], sw2v.at[1, half], 19, dev_d)
    y_hid = remote(hyo, hsi, 20, dev_y)
    x_tok, f_tok = [], []
    for k in range(NK):
        cols = part(k, KC)
        x_tok.append([remote(toks[m].at[:, cols], tok.at[2, m, :, cols], 21 + 2 * k + m, dev_x) for m in range(2)])
        f_tok.append([remote(tok.at[2, m, :, cols], tok.at[3, m, :, cols], 21 + 2 * NK + 2 * k + m, dev_d)
                      for m in range(2)])
    base_sem = 21 + 4 * NK

    def block(kind, m, c):
        return pf.at[pl.ds((kind * 2 * NCH + 2 * c + m) * TOK, TOK), pl.ds(0, CHS[c])]

    def send_r(m, c):
        return block(0, m, c)

    def send_l(m, c):
        return block(1, m, c)

    def send_x(m, c):
        return block(2, m, c)

    def kept(m, c):
        return block(3, m, c)

    def d_rem(m, c):
        return remote(send_r(m, c), recvr.at[m, :, out_cols(c)], base_sem + 2 * c + m, dev_d)

    def d_loc(m, c):
        return remote(send_l(m, c), recvl.at[m, :, out_cols(c)], base_sem + 2 * NCH + 2 * c + m, dev_d)

    def x_part(m, c):
        return remote(send_x(m, c), xr.at[m, :, out_cols(c)], base_sem + 4 * NCH + 2 * c + m, dev_x)

    def swiglu(rows, w1, w3):
        p1 = dot(rows, w1)
        p3 = dot(rows, w3)
        return (jax.nn.silu(p1) * p3).astype(BF16)

    def build(src):
        def rows_of(i, _):
            m, b = i // (SROWS // 128), i % (SROWS // 128)
            at = part(b, 128)
            slot = mi[src, 2 * m + 1]
            el = mi[src, 2 * m] - first
            ok = (slot >= 0) & (el >= 0) & (el < NE)
            rid = jnp.where(ok, el * CAP + slot, -1) - b * 128
            g = mg[src, m]
            row = lax.broadcasted_iota(jnp.int32, (128, TOK), 0)
            hit = jnp.zeros((128, TOK), F32)
            gt = jnp.zeros((128, TOK), F32)
            for j in range(TOPK):
                same = row == rid[j:j + 1, :]
                hit = jnp.where(same, 1.0, hit)
                gt = jnp.where(same, g[j:j + 1, :], gt)
            pmat[2 * src + m, at, :] = hit.astype(BF16)
            gg = gt.T
            hi = jnp.minimum(gg, BF16_MAX).astype(BF16)
            r1 = gg - hi.astype(F32)
            mid = r1.astype(BF16)
            lo = (r1 - mid.astype(F32)).astype(BF16)
            for k, v in enumerate((hi, mid, lo)):
                g3[2 * src + m, k * TOK:(k + 1) * TOK, at] = v
            return 0
        lax.fori_loop(0, 2 * SROWS // 128, rows_of, 0)

    def dispatch(k, src):
        cols = part(k, KC)
        r0 = dot(pmat[2 * src], tok[src, 0, :, cols])
        r1 = dot(pmat[2 * src + 1], tok[src, 1, :, cols])
        for e in range(NE):
            both = jnp.concatenate([r0[e * CAP:(e + 1) * CAP], r1[e * CAP:(e + 1) * CAP]], axis=0)
            at = e * ROWS + src * 2 * CAP
            buf[at:at + 2 * CAP, :] = both.astype(BF16)

    def stage1(k):
        per = 4

        def step(i, _):
            for u in range(per):
                n = k * NE + per * i + u
                for c in first_item(n, n % NS):
                    c.wait()
            for u in range(per):
                e = per * i + u
                slot = (k * NE + e) % NS
                rows = buf[part(e, ROWS), :]
                p1 = dot(rows, ring[slot, :KC])
                p3 = dot(rows, ring[slot, KC:])
                at1, at3 = part(2 * e, ROWS), part(2 * e + 1, ROWS)
                if k:
                    p1 = p1 + pf[at1, :]
                    p3 = p3 + pf[at3, :]
                if k < NK - 1:
                    pf[at1, :] = p1
                    pf[at3, :] = p3
                else:
                    hid[e] = (jax.nn.silu(p1) * p3).astype(BF16)
            for u in range(per):
                refill(k * NE + per * i + u + NS, k * NE + NS, (k + 1) * NE + NS)
            return 0
        lax.fori_loop(0, NE // per, step, 0)

    def combine(s, w):
        q = dot(g3[s], buf[s * SROWS:(s + 1) * SROWS, :w])
        return q[:TOK] + q[TOK:2 * TOK] + q[2 * TOK:]

    def stage2(c):
        w = CHS[c]
        per_row = FF // w
        items = 2 // per_row

        def step(q, _):
            r = []
            for i in range(items):
                for d in second_item(c, q * items + i, (ITEM2[c] + q * items + i) % NS):
                    d.wait()
            for i in range(4):
                slot = (ITEM2[c] + q * items + i // (4 // items)) % NS
                j = i % (4 // items)
                a, b = (j // per_row) * FF, (j % per_row) * w
                r.append(dot(hid[4 * q + i], ring[slot, a:a + FF, b:b + w]))
            for s in range(SRC):
                rows = jnp.concatenate([v[s * CAP:(s + 1) * CAP] for v in r], axis=0)
                buf[pl.ds(pl.multiple_of(s * SROWS + q * 4 * CAP, 4 * CAP), 4 * CAP), :w] = rows.astype(BF16)
            for i in range(items):
                low = ITEM2[c] + NS
                refill(ITEM2[c] + q * items + i + NS, low, low + 4 * items)
            return 0
        lax.fori_loop(0, 4, step, 0)

        for m in range(2):
            send_r(m, c)[...] = combine(6 + m, w)
            d_rem(m, c).start()
        for m in range(2):
            send_x(m, c)[...] = combine(4 + m, w)
        for m in range(2):
            send_l(m, c)[...] = combine(2 + m, w)
            d_loc(m, c).start()
        for m in range(2):
            d_rem(m, c).wait_recv()
            send_x(m, c)[...] = send_x(m, c)[...] + recvr[m, :, COL[c]:COL[c] + w]
            x_part(m, c).start()
        for m in range(2):
            kept(m, c)[...] = combine(m, w)

    for c in own_meta + own_tok:
        c.start()
    barrier = pltpu.get_barrier_semaphore()
    for dev in (dev_d, dev_x, dev_y):
        pl.semaphore_signal(barrier, inc=1, device_id=dev, device_id_type=MESH)
    pl.semaphore_wait(barrier, 3)
    for c in x_meta + d_meta + x_tok[0] + d_tok + x_tok[1] + x_tok[2] + y_tok + [y_w2]:
        c.start()
    for c in own_meta + own_tok:
        c.wait()
    for c in shared[:2]:
        c.start()

    def fill(n, _):
        for c in first_item(n, n):
            c.start()
        return 0
    lax.fori_loop(0, NS, fill, 0)
    shared[2].start()

    build(0)
    for c in d_meta + x_meta:
        c.wait_recv()
    for c in f_meta:
        c.start()
    build(1)
    build(2)
    for c in f_meta + d_tok:
        c.wait_recv()
    build(3)
    for c in shared[:2]:
        c.wait()
    for m in range(2):
        hso[m] = swiglu(tok[0, m], sw13[0], sw13[1])

    for k in range(NK):
        if k == 0:
            dispatch(k, 0)
            dispatch(k, 1)
        for c in x_tok[k]:
            c.wait_recv()
        for c in f_tok[k]:
            c.start()
        if k:
            dispatch(k, 0)
            dispatch(k, 1)
        dispatch(k, 2)
        for c in f_tok[k]:
            c.wait_recv()
        dispatch(k, 3)
        stage1(k)

    for c in range(NCH):
        stage2(c)
        if c == 1:
            for d in y_tok:
                d.wait_recv()
            for m in range(2):
                hyo[m] = swiglu(ytok[m * TOK:(m + 1) * TOK], sw13[0], sw13[1])
            y_hid.start()
    y_w2.wait_recv()
    f_w2.start()
    shared[2].wait()
    f_w2.wait_recv()
    y_hid.wait_recv()

    for c in range(NCH):
        at = slice(COL[c], COL[c] + CHS[c])
        for m in range(2):
            d_loc(m, c).wait_recv()
            s = dot(hso[m], sw2v[0, :, at]) + dot(hsi[m], sw2v[1, :, at])
            kept(m, c)[...] = kept(m, c)[...] + recvl[m, :, at] + s + tok[0, m, :, at].astype(F32)
    for c in range(NCH):
        at = slice(COL[c], COL[c] + CHS[c])
        for m in range(2):
            x_part(m, c).wait_recv()
            ost[m, :, at] = (kept(m, c)[...] + xr[m, :, at]).astype(BF16)
            put(m, c).start()

    for c in x_meta + d_meta + f_meta + d_tok + y_tok + [y_w2, f_w2, y_hid] + sum(x_tok, []) + sum(f_tok, []):
        c.wait_send()
    for c in range(NCH):
        for m in range(2):
            d_rem(m, c).wait_send()
            d_loc(m, c).wait_send()
            x_part(m, c).wait_send()
            put(m, c).wait()


def solution(mesh):
    tok_spec = P(('data', 'ep', 'tp'), None)
    in_specs = (tok_spec,) * 8 + (P(None, 'tp'), P(None, 'tp'), P('tp', None), P('ep', None, None), P('ep', None, None), P('ep', None, None))
    nsem = 21 + 4 * NK + 6 * NCH
    scratch = [
        pltpu.VMEM((NS, 2 * KC, FF), BF16),
        pltpu.VMEM((2, DIM, FF), BF16),
        pltpu.VMEM((2, FF, DIM), BF16),
        pltpu.VMEM((4, 2, TOK, DIM), BF16),
        pltpu.VMEM((2 * TOK, DIM), BF16),
        pltpu.VMEM((NE * ROWS, KC), BF16),
        pltpu.VMEM((2 * NE * ROWS, FF), F32),
        pltpu.VMEM((NE, ROWS, FF), BF16),
        pltpu.VMEM((SRC, SROWS, TOK), BF16),
        pltpu.VMEM((SRC, 3 * TOK, SROWS), BF16),
        pltpu.VMEM((2, TOK, DIM), F32),
        pltpu.VMEM((2, TOK, DIM), F32),
        pltpu.VMEM((2, TOK, DIM), F32),
        pltpu.VMEM((2, TOK, FF), BF16),
        pltpu.VMEM((2, TOK, FF), BF16),
        pltpu.VMEM((2, TOK, FF), BF16),
        pltpu.VMEM((2, TOK, DIM), BF16),
        pltpu.VMEM((4, 4, TOPK, TOK), jnp.int32),
        pltpu.VMEM((4, 2, TOPK, TOK), F32),
        pltpu.SemaphoreType.DMA((11 + 2 * NCH,)),
        pltpu.SemaphoreType.DMA((NS, 4)),
        pltpu.SemaphoreType.DMA((nsem,)),
        pltpu.SemaphoreType.DMA((nsem,)),
    ]

    def layer_local(tokens_a, tokens_b, experts_a, experts_b, gates_a, gates_b, slots_a, slots_b, shared_w1, shared_w3, shared_w2, routed_w1, routed_w3, routed_w2):
        both = pl.pallas_call(
            kernel,
            out_shape=jax.ShapeDtypeStruct((2, TOK, DIM), BF16),
            in_specs=[pl.BlockSpec(memory_space=pl.ANY)] * 14,
            out_specs=pl.BlockSpec(memory_space=pl.ANY),
            scratch_shapes=scratch,
            compiler_params=pltpu.CompilerParams(collective_id=0, has_side_effects=True, vmem_limit_bytes=67043328),
        )(tokens_a, tokens_b, experts_a.T, slots_a.T, experts_b.T, slots_b.T, gates_a.T, gates_b.T,
          shared_w1, shared_w3, shared_w2, routed_w1, routed_w3, routed_w2)
        return both[0], both[1]

    return jax.shard_map(layer_local, mesh=mesh, in_specs=in_specs, out_specs=(tok_spec, tok_spec), check_vma=False)
```

time: 80.3 us -> 73.9 us (0.920)
  Pallas kernels: 75.9 us -> 71.1 us
  local copies, waits for them, and re-layouts: 3.53 us -> 2.04 us
    pallas_call x1, Pallas kernels: 75.9 us -> 71.1 us  [layer_local(): pl.pallas_call(kernel, out_shape=jax.ShapeDtypeStruct((2, TOK, DIM), BF16...]
    unnamed x2 -> x0, local copies, waits for them, and re-layouts: 3.53 us -> none
    squeeze x0 -> x1, local copies, waits for them, and re-layouts: none -> 2.04 us  [layer_local(): return (both[0], both[1])]
where the time goes in v3:
time: 73.9 us; the launch traced here: 73.8 us
  Pallas kernels  71.1 us (96%)
  local copies, waits for them, and re-layouts  2.04 us (3%)
    pallas_call x1, Pallas kernels, layer_local(): pl.pallas_call(kernel, out_shape=jax.ShapeDtypeStruct((2, TOK, DIM), BF16...  71.1 us
    squeeze x1, local copies, waits for them, and re-layouts, layer_local(): return (both[0], both[1])  2.04 us

profile of v3, /device:TPU:0, one launch (start us, length us, event | category | flops | bytes accessed | tf_op | source)
XLA Modules:
  0.0 73.8 jit_solution(5151184740876336202)
XLA Ops:
  0.6 71.1 %shard_map.149 = bf16[2,128,1536]{2,1,0:T(8,128)(2,1)} custom-call(bf16[128,1536]{1,0:T(8,128)(2,1)} %tok_a.1, bf16[128,1536]{1,0:T(8,128)(2,1)} %tok_b.1, s32[6,128]{1,0:T(8,128)} %bitcast.10, s32[6,128]{1,0:T(8,128)} %bitcast.11, s32[6,128]{1,0:T(8,128)} %bitcast.12, s32[6,128]{1,0:T(8,128)} %bitcast.13, f32[6,128]{1,0:T(8,128)} %bitcast.14, ...), custom_call_target="tpu_custom_call" | custom-call | tf_op jit(solution)/shard_map/pallas_call | solution.py:382
  71.8 2.0 %slice_bitcast_fusion = (bf16[128,1536]{1,0:T(8,128)(2,1)}, bf16[128,1536]{1,0:T(8,128)(2,1)}) fusion(bf16[2,128,1536]{2,1,0:T(8,128)(2,1)} %shard_map.149), kind=kLoop, calls=%fused_computation | loop fusion | bytes 1572864 | tf_op jit(solution)/shard_map/squeeze | solution.py:391

commit v4 on v3

v4 whole, which is shorter than its diff:
```python
import functools

import jax
import jax.numpy as jnp
from jax import lax
from jax.experimental import pallas as pl
from jax.experimental.pallas import tpu as pltpu
from jax.sharding import PartitionSpec as P

MESH = pl.DeviceIdType.MESH
F32, BF16 = jnp.float32, jnp.bfloat16

TOK = 128
DIM = 1536
FF = 512
TOPK = 6
CAP = 24
NE = 16
SRC = 4
ROWS = SRC * CAP
SROWS = NE * CAP
KC = 512
NK = DIM // KC
CH = 256
NCH = DIM // CH
EARLY = 3
NS = 24
N1 = NK * NE
BF16_MAX = 3.3895313892515355e38


def dot(a, b):
    return jnp.dot(a, b, preferred_element_type=F32)


def kernel(tok_a, tok_b, e_a, s_a, e_b, s_b, g_a, g_b, sw1, sw3, sw2, rw1, rw3, rw2,
           out_ab, out_kept, out_x,
           ring, sw13, sw2v, tok, ytok, buf, pf, hid, pmat, g3,
           recvr, recvl, xr, hso, hyo, hsi, ost, mi, mg,
           loc_sem, ring_sem, snd, rcv):
    tp = lax.axis_index('tp')
    ep = lax.axis_index('ep')
    core = lax.rem(ep, 2)
    first = ep * NE
    dev_d = {'ep': ep + 1 - 2 * core}
    dev_x = {'ep': lax.rem(ep + 2, 4)}
    dev_y = {'tp': 1 - tp}
    toks, ids, gates = (tok_a, tok_b), (e_a, s_a, e_b, s_b), (g_a, g_b)

    def local(src, dst, sem):
        return pltpu.make_async_copy(src, dst, loc_sem.at[sem])

    def remote(src, dst, sem, dev):
        return pltpu.make_async_remote_copy(src_ref=src, dst_ref=dst, send_sem=snd.at[sem], recv_sem=rcv.at[sem],
                                            device_id=dev, device_id_type=MESH)

    def mult(i, k):
        return i * k if isinstance(i, int) else pl.multiple_of(i * k, k)

    def part(i, k):
        return pl.ds(mult(i, k), k)

    own = [local(ids[i], mi.at[0, i], 0) for i in range(4)] + [local(gates[m], mg.at[0, m], 1) for m in range(2)]
    own += [local(toks[m], tok.at[0, m], 2) for m in range(2)]
    own_all = [local(mi.at[1], mi.at[0], 0), local(mg.at[1], mg.at[0], 1), local(tok.at[1], tok.at[0], 2)]
    shared = [local(sw1, sw13.at[0], 3), local(sw3, sw13.at[1], 4), local(sw2, sw2v.at[0], 5)]

    def out_cols(c):
        return part(c, CH)

    def put(m, c):
        if c == NCH - 1:
            return local(kept(m, c), out_kept.at[m], 6)
        return local(ost.at[m, :, out_cols(c)], out_ab.at[m, :, out_cols(c)], 7)

    def first_item(n, slot):
        e, rows = n % NE, part(n // NE, KC)
        return (pltpu.make_async_copy(rw1.at[e, rows], ring.at[slot, pl.ds(0, KC)], ring_sem.at[slot]),
                pltpu.make_async_copy(rw3.at[e, rows], ring.at[slot, pl.ds(KC, KC)], ring_sem.at[slot]))

    def second_item(c, q, slot):
        return [pltpu.make_async_copy(rw2.at[4 * q + i, :, out_cols(c)],
                                      ring.at[slot, pl.ds((i // 2) * FF, FF), pl.ds((i % 2) * CH, CH)],
                                      ring_sem.at[slot]) for i in range(4)]

    def load2(c, slot0):
        def go(q, _):
            for d in second_item(c, q, slot0 + q):
                d.start()
            return 0
        lax.fori_loop(0, NE // 4, go, 0)

    def wait_item(slot):
        pltpu.make_async_copy(rw1.at[0, pl.ds(0, 2 * KC)], ring.at[slot], ring_sem.at[slot]).wait()

    def refill(n, low, high):
        def one():
            for d in first_item(n, n % NS):
                d.start()

        def two():
            for d in second_item((n - N1) // 4, (n - N1) % 4, n % NS):
                d.start()
        if high <= N1:
            one()
        elif low >= N1:
            two()
        else:
            pl.when(n < N1)(one)
            pl.when(n >= N1)(two)

    def same(ref, sem, dev):
        return remote(ref, ref, sem, dev)

    d_meta = [remote(ids[i], mi.at[1, i], 0, dev_d) for i in range(4)] + [remote(gates[m], mg.at[1, m], 1, dev_d) for m in range(2)]
    d_meta_all = [same(mi.at[1], 0, dev_d), same(mg.at[1], 1, dev_d)]
    x_meta = [remote(ids[i], mi.at[2, i], 2, dev_x) for i in range(4)] + [remote(gates[m], mg.at[2, m], 3, dev_x) for m in range(2)]
    x_meta_all = [same(mi.at[2], 2, dev_x), same(mg.at[2], 3, dev_x)]
    f_meta = [remote(mi.at[2], mi.at[3], 4, dev_d), remote(mg.at[2], mg.at[3], 5, dev_d)]
    d_tok = [remote(toks[m], tok.at[1, m], 6, dev_d) for m in range(2)]
    d_tok_all = same(tok.at[1], 6, dev_d)
    y_tok = [remote(toks[m], ytok.at[pl.ds(m * TOK, TOK)], 7, dev_y) for m in range(2)]
    y_tok_all = same(ytok, 7, dev_y)
    half = part(core, FF // 2)
    y_w2 = remote(sw2.at[half], sw2v.at[1, half], 8, dev_y)
    f_w2 = remote(sw2v.at[1, half], sw2v.at[1, half], 9, dev_d)
    y_hid = remote(hyo, hsi, 10, dev_y)
    x_tok, f_tok = [], []
    for k in range(NK):
        cols = part(k, KC)
        x_tok.append([remote(toks[m].at[:, cols], tok.at[2, m, :, cols], 11 + 2 * k + m, dev_x) for m in range(2)])
        f_tok.append([remote(tok.at[2, m, :, cols], tok.at[3, m, :, cols], 11 + 2 * NK + 2 * k + m, dev_d) for m in range(2)])
    base_sem = 11 + 4 * NK
    loc_of = base_sem + NCH + EARLY

    def block(kind, m, c):
        return pf.at[m, pl.ds((kind * NCH + c) * TOK, TOK), pl.ds(0, CH)]

    def send_r(m, c):
        return block(0, m, c)

    def send_l(m, c):
        return block(1, m, c)

    def send_x(m, c):
        return block(2, m, c)

    def kept(m, c):
        return block(3, m, c)

    def d_rem(m, c):
        return remote(send_r(m, c), recvr.at[m, :, out_cols(c)], base_sem + (2 * c + m if c < EARLY else c + EARLY), dev_d)

    def d_rem_all(c, ms):
        if len(ms) == 1:
            return d_rem(ms[0], c)
        return same(recvr.at[:, :, out_cols(c)], base_sem + c + EARLY, dev_d)

    def d_loc(m, c):
        return remote(send_l(m, c), recvl.at[m, :, out_cols(c)], loc_of, dev_d)

    d_loc_all = same(recvl, loc_of, dev_d)

    def x_part(m, c):
        to = out_x.at[m] if c == NCH - 1 else xr.at[m, :, out_cols(c)]
        return remote(send_x(m, c), to, loc_of + 1 + max(c - (NCH - 3), 0), dev_x)

    x_part_all = [same(xr.at[:, :, pl.ds(0, (NCH - 2) * CH)], loc_of + 1, dev_x),
                  same(xr.at[:, :, out_cols(NCH - 2)], loc_of + 2, dev_x),
                  same(out_x, loc_of + 3, dev_x)]

    def swiglu(rows, w1, w3):
        p1 = dot(rows, w1)
        p3 = dot(rows, w3)
        return (jax.nn.silu(p1) * p3).astype(BF16)

    def build(src):
        def rows_of(i, _):
            m, b = i // (SROWS // 128), i % (SROWS // 128)
            at = part(b, 128)
            slot = mi[src, 2 * m + 1]
            el = mi[src, 2 * m] - first
            ok = (slot >= 0) & (el >= 0) & (el < NE)
            rid = jnp.where(ok, el * CAP + slot, -1) - b * 128
            g = mg[src, m]
            row = lax.broadcasted_iota(jnp.int32, (128, TOK), 0)
            hit = jnp.zeros((128, TOK), F32)
            gt = jnp.zeros((128, TOK), F32)
            for j in range(TOPK):
                same = row == rid[j:j + 1, :]
                hit = jnp.where(same, 1.0, hit)
                gt = jnp.where(same, g[j:j + 1, :], gt)
            pmat[SRC * m + src, at, :] = hit.astype(BF16)
            gg = gt.T
            hi = jnp.minimum(gg, BF16_MAX).astype(BF16)
            r1 = gg - hi.astype(F32)
            mid = r1.astype(BF16)
            lo = (r1 - mid.astype(F32)).astype(BF16)
            for k, v in enumerate((hi, mid, lo)):
                g3[SRC * m + src, k * TOK:(k + 1) * TOK, at] = v
            return 0
        lax.fori_loop(0, 2 * SROWS // 128, rows_of, 0)

    def dispatch(k, m, pair):
        cols = part(k, KC)
        r0 = dot(pmat[SRC * m + 2 * pair], tok[2 * pair, m, :, cols])
        r1 = dot(pmat[SRC * m + 2 * pair + 1], tok[2 * pair + 1, m, :, cols])
        for e in range(NE):
            both = jnp.concatenate([r0[e * CAP:(e + 1) * CAP], r1[e * CAP:(e + 1) * CAP]], axis=0)
            at = e * ROWS + pair * 2 * CAP
            buf[m, at:at + 2 * CAP, :] = both.astype(BF16)

    def load(ref, ms, at):
        return jnp.concatenate([ref[m, at, :] for m in ms], axis=0) if len(ms) > 1 else ref[ms[0], at, :]

    def stage1(k, ms, half=None, fresh=True, done=True):
        per = 8 if k < NK - 1 else 16

        def step(i, _):
            if fresh:
                for u in range(per):
                    wait_item((k * NE + per * i + u) % NS)
            for u in range(per):
                e = per * i + u
                slot = (k * NE + e) % NS
                rows = load(buf, ms, part(e, ROWS))
                p1 = dot(rows, ring[slot, :KC])
                p3 = dot(rows, ring[slot, KC:])
                at1, at3 = part(2 * e, ROWS), part(2 * e + 1, ROWS)
                if k:
                    p1 = p1 + load(pf, ms, at1)
                    p3 = p3 + load(pf, ms, at3)
                if k == NK - 1:
                    p1 = (jax.nn.silu(p1) * p3).astype(BF16)
                for j, m in enumerate(ms):
                    at = slice(j * ROWS, (j + 1) * ROWS)
                    if k < NK - 1:
                        pf[m, at1, :] = p1[at]
                        pf[m, at3, :] = p3[at]
                    else:
                        hid[m, e] = p1[at]
            if done:
                for u in range(per):
                    low = k * NE + NS if half is None else k * NE + NS + half * NE // 2
                    high = (k + 1) * NE + NS if half is None else low + NE // 2
                    refill(k * NE + per * i + u + NS, low, high)
            return 0
        if half is None:
            lax.fori_loop(0, NE // per, step, 0)
        else:
            lax.fori_loop(half * NE // per // 2, (half + 1) * NE // per // 2, step, 0)

    def combine(m, s):
        q = dot(g3[SRC * m + s], buf[m, s * SROWS:(s + 1) * SROWS, :CH])
        return q[:TOK] + q[TOK:2 * TOK] + q[2 * TOK:]

    def stage2(c, ms, slot0, fresh=True):
        loop = 2 if len(ms) > 1 else 4

        def step(q, _):
            r = []
            if fresh:
                for i in range(loop):
                    wait_item(slot0 + q * loop + i)
            for i in range(4 * loop):
                slot = slot0 + q * loop + i // 4
                a, b = (i % 4 // 2) * FF, (i % 2) * CH
                e = 4 * loop * q + i
                rows = jnp.concatenate([hid[m, e] for m in ms], axis=0) if len(ms) > 1 else hid[ms[0], e]
                r.append(dot(rows, ring[slot, a:a + FF, b:b + CH]))
            for j, m in enumerate(ms):
                for s in range(SRC):
                    low = j * ROWS + s * CAP
                    rows = jnp.concatenate([v[low:low + CAP] for v in r], axis=0)
                    k = 4 * CAP * loop
                    buf[m, pl.ds(pl.multiple_of(s * SROWS + q * k, 2 * CAP), k), :CH] = rows.astype(BF16)
            return 0
        lax.fori_loop(0, 4 // loop, step, 0)

        to_die = [combine(m, 3) for m in ms]
        to_x = [combine(m, 2) for m in ms]
        for m, v in zip(ms, to_die):
            send_r(m, c)[...] = v
            d_rem(m, c).start()
        for m, v in zip(ms, to_x):
            send_x(m, c)[...] = v
        to_die = [combine(m, 1) for m in ms]
        home = [combine(m, 0) for m in ms]
        for m, v in zip(ms, to_die):
            send_l(m, c)[...] = v
            d_loc(m, c).start()
        for m, v in zip(ms, home):
            kept(m, c)[...] = v

    def pass_on(c, ms):
        d_rem_all(c, ms).wait_recv()
        for m in ms:
            send_x(m, c)[...] = send_x(m, c)[...] + recvr[m, :, c * CH:(c + 1) * CH]
            x_part(m, c).start()

    def arrived(k, ms):
        for m in ms:
            x_tok[k][m].wait_recv()
            f_tok[k][m].start()

    barrier = pltpu.get_barrier_semaphore()
    for dev in (dev_d, dev_x, dev_y):
        pl.semaphore_signal(barrier, inc=1, device_id=dev, device_id_type=MESH)
    for c in own:
        c.start()

    def fill(n, _):
        for c in first_item(n, n):
            c.start()
        return 0
    lax.fori_loop(0, 8, fill, 0)
    pl.semaphore_wait(barrier, 3)
    for c in x_meta + d_meta + x_tok[0] + d_tok + x_tok[1] + x_tok[2] + y_tok + [y_w2]:
        c.start()
    lax.fori_loop(8, NS, fill, 0)
    for c in own_all:
        c.wait()

    build(0)
    for c in d_meta_all + x_meta_all:
        c.wait_recv()
    for c in f_meta:
        c.start()
    build(1)
    build(2)
    for c in f_meta + [d_tok_all]:
        c.wait_recv()
    build(3)

    both, a, b = (0, 1), (0,), (1,)
    for m in both:
        dispatch(0, m, 0)
    arrived(0, a)
    arrived(0, b)
    for m in both:
        f_tok[0][m].wait_recv()
        dispatch(0, m, 1)
    stage1(0, both)
    arrived(1, a)
    dispatch(1, 0, 0)
    arrived(1, b)
    dispatch(1, 1, 0)
    for m in both:
        f_tok[1][m].wait_recv()
        dispatch(1, m, 1)
    stage1(1, both, half=0)
    arrived(2, a)
    stage1(1, both, half=1)
    dispatch(2, 0, 0)
    f_tok[2][0].wait_recv()
    dispatch(2, 0, 1)
    stage1(2, a, done=False)
    arrived(2, b)

    stage2(0, a, 0)
    load2(2, 0)
    dispatch(2, 1, 0)
    pass_on(0, a)
    stage2(1, a, 4)
    f_tok[2][1].wait_recv()
    dispatch(2, 1, 1)
    pass_on(1, a)
    stage2(2, a, 0)
    for c in shared:
        c.start()
    pass_on(2, a)
    stage1(2, b, fresh=False, done=False)
    load2(0, 8)
    load2(3, 12)
    load2(4, 16)
    load2(5, 20)
    stage2(1, b, 4, fresh=False)
    pass_on(1, b)
    stage2(2, b, 0, fresh=False)
    pass_on(2, b)
    stage2(0, b, 8)
    pass_on(0, b)
    stage2(3, both, 12)
    pass_on(3, both)
    for c in shared:
        c.wait()
    y_tok_all.wait_recv()
    for m in both:
        hyo[m] = swiglu(ytok[m * TOK:(m + 1) * TOK], sw13[0], sw13[1])
    y_hid.start()
    stage2(4, both, 16)
    pass_on(4, both)
    stage2(5, both, 20)
    pass_on(5, both)
    for m in both:
        hso[m] = swiglu(tok[0, m], sw13[0], sw13[1])
    y_w2.wait_recv()
    f_w2.start()
    y_hid.wait_recv()
    d_loc_all.wait_recv()
    f_w2.wait_recv()

    for c in range(NCH - 1, -1, -1):
        at = slice(c * CH, (c + 1) * CH)
        for m in both:
            s = dot(hso[m], sw2v[0, :, at]) + dot(hsi[m], sw2v[1, :, at])
            kept(m, c)[...] = kept(m, c)[...] + recvl[m, :, at] + s + tok[0, m, :, at].astype(F32)
            if c == NCH - 1:
                put(m, c).start()
    for c in range(NCH - 1):
        at = slice(c * CH, (c + 1) * CH)
        if c == 0 or c == NCH - 2:
            x_part_all[min(c, 1)].wait_recv()
        for m in both:
            ost[m, :, at] = (kept(m, c)[...] + xr[m, :, at]).astype(BF16)
            put(m, c).start()

    for c in x_meta_all + d_meta_all + f_meta + [d_tok_all, y_tok_all, y_w2, f_w2, y_hid, d_loc_all]:
        c.wait_send()
    for c in sum(x_tok, []) + sum(f_tok, []) + x_part_all:
        c.wait_send()
    for c in range(NCH):
        for ms in ((both,) if c >= EARLY else (a, b)):
            d_rem_all(c, ms).wait_send()
    local(recvl.at[:, :, out_cols(NCH - 1)], out_kept, 6).wait()
    local(ost.at[:, :, pl.ds(0, DIM - CH)], out_ab.at[:, :, pl.ds(0, DIM - CH)], 7).wait()
    x_part_all[2].wait_recv()


def finish(most, kept, x, out_a, out_b, row, k_v, x_v, sem):
    ready = DIM - CH
    early = [pltpu.make_async_copy(most.at[m, :, pl.ds(0, ready)], row.at[m, :, pl.ds(0, ready)], sem.at[m]) for m in range(2)]
    late = [pltpu.make_async_copy(kept.at[m], k_v.at[m], sem.at[2 + m]) for m in range(2)]
    late += [pltpu.make_async_copy(x.at[m], x_v.at[m], sem.at[4 + m]) for m in range(2)]
    for c in late + early:
        c.start()
    for c in late:
        c.wait()
    for m in range(2):
        row[m, :, ready:] = (k_v[m] + x_v[m]).astype(BF16)
    back = []
    for m, out in enumerate((out_a, out_b)):
        early[m].wait()
        back.append(pltpu.make_async_copy(row.at[m], out, sem.at[6 + m]))
        back[m].start()
    for c in back:
        c.wait()


def solution(mesh):
    tok_spec = P(('data', 'ep', 'tp'), None)
    in_specs = (tok_spec,) * 8 + (P(None, 'tp'), P(None, 'tp'), P('tp', None), P('ep', None, None), P('ep', None, None), P('ep', None, None))
    nsem = 11 + 4 * NK + NCH + EARLY + 4
    scratch = [
        pltpu.VMEM((NS, 2 * KC, FF), BF16),
        pltpu.VMEM((2, DIM, FF), BF16),
        pltpu.VMEM((2, FF, DIM), BF16),
        pltpu.VMEM((4, 2, TOK, DIM), BF16),
        pltpu.VMEM((2 * TOK, DIM), BF16),
        pltpu.VMEM((2, NE * ROWS, KC), BF16),
        pltpu.VMEM((2, 2 * NE * ROWS, FF), F32),
        pltpu.VMEM((2, NE, ROWS, FF), BF16),
        pltpu.VMEM((2 * SRC, SROWS, TOK), BF16),
        pltpu.VMEM((2 * SRC, 3 * TOK, SROWS), BF16),
        pltpu.VMEM((2, TOK, DIM), F32),
        pltpu.VMEM((2, TOK, DIM), F32),
        pltpu.VMEM((2, TOK, DIM), F32),
        pltpu.VMEM((2, TOK, FF), BF16),
        pltpu.VMEM((2, TOK, FF), BF16),
        pltpu.VMEM((2, TOK, FF), BF16),
        pltpu.VMEM((2, TOK, DIM), BF16),
        pltpu.VMEM((4, 4, TOPK, TOK), jnp.int32),
        pltpu.VMEM((4, 2, TOPK, TOK), F32),
        pltpu.SemaphoreType.DMA((8,)),
        pltpu.SemaphoreType.DMA((NS,)),
        pltpu.SemaphoreType.DMA((nsem,)),
        pltpu.SemaphoreType.DMA((nsem,)),
    ]

    def layer_local(tokens_a, tokens_b, experts_a, experts_b, gates_a, gates_b, slots_a, slots_b, shared_w1, shared_w3, shared_w2, routed_w1, routed_w3, routed_w2):
        hbm = pl.BlockSpec(memory_space=pl.ANY)
        tail = jax.ShapeDtypeStruct((2, TOK, CH), F32)
        parts = pl.pallas_call(
            kernel,
            out_shape=(jax.ShapeDtypeStruct((2, TOK, DIM), BF16), tail, tail),
            in_specs=[hbm] * 14,
            out_specs=(hbm,) * 3,
            scratch_shapes=scratch,
            compiler_params=pltpu.CompilerParams(collective_id=0, has_side_effects=True, vmem_limit_bytes=67043328),
        )(tokens_a, tokens_b, experts_a.T, slots_a.T, experts_b.T, slots_b.T, gates_a.T, gates_b.T,
          shared_w1, shared_w3, shared_w2, routed_w1, routed_w3, routed_w2)
        return pl.pallas_call(
            finish,
            out_shape=(jax.ShapeDtypeStruct((TOK, DIM), BF16),) * 2,
            in_specs=[hbm] * 3,
            out_specs=(hbm,) * 2,
            scratch_shapes=[pltpu.VMEM((2, TOK, DIM), BF16), pltpu.VMEM((2, TOK, CH), F32),
                            pltpu.VMEM((2, TOK, CH), F32), pltpu.SemaphoreType.DMA((8,))],
        )(*parts)

    return jax.shard_map(layer_local, mesh=mesh, in_specs=in_specs, out_specs=(tok_spec, tok_spec), check_vma=False)
```

time: 73.9 us -> 69.9 us (0.946)
  Pallas kernels: 71.1 us -> 69 us
  local copies, waits for them, and re-layouts: 2.04 us -> 0 us
    pallas_call x1 -> x2, Pallas kernels: 71.1 us -> 69 us  [the longest x1 66.8 us: layer_local(): pl.pallas_call(kernel, out_shape=(jax.ShapeDtypeStruct((2, TOK, DIM), BF1...]
    squeeze x1 -> x0, local copies, waits for them, and re-layouts: 2.04 us -> none  [layer_local(): return (both[0], both[1])]
where the time goes in v4:
time: 69.9 us; the launch traced here: 69.8 us
  Pallas kernels  69 us (99%)
  between operations  0.82 us (1%)
    pallas_call x1, Pallas kernels, layer_local(): pl.pallas_call(kernel, out_shape=(jax.ShapeDtypeStruct((2, TOK, DIM), BF1...  66.8 us
    pallas_call x1, Pallas kernels, layer_local(): pl.pallas_call(finish, out_shape=(jax.ShapeDtypeStruct((TOK, DIM), BF16),...  2.18 us

profile of v4, /device:TPU:0, one launch (start us, length us, event | category | flops | bytes accessed | tf_op | source)
XLA Modules:
  0.0 69.8 jit_solution(5192749405756601204)
XLA Ops:
  0.6 66.8 %shard_map.149 = (bf16[2,128,1536]{2,1,0:T(8,128)(2,1)}, f32[2,128,256]{2,1,0:T(8,128)}, f32[2,128,256]{2,1,0:T(8,128)}) custom-call(bf16[128,1536]{1,0:T(8,128)(2,1)} %tok_a.1, bf16[128,1536]{1,0:T(8,128)(2,1)} %tok_b.1, s32[6,128]{1,0:T(8,128)} %bitcast.6, s32[6,128]{1,0:T(8,128)} %bitcast.7, s32[6,128]{1,0:T(8,128)} %bitcast.8, s32[6,128]{1,0:T(8,128)} %bitcast.9, ...), custom_call_target="tpu_custom_call" | custom-call | tf_op jit(solution)/shard_map/pallas_call | solution.py:483
  67.4 2.2 %shard_map.150 = (bf16[128,1536]{1,0:T(8,128)(2,1)}, bf16[128,1536]{1,0:T(8,128)(2,1)}) custom-call(bf16[2,128,1536]{2,1,0:T(8,128)(2,1)} %get-tuple-element.5.most, f32[2,128,256]{2,1,0:T(8,128)} %get-tuple-element.6.kept, f32[2,128,256]{2,1,0:T(8,128)} %get-tuple-element.7.x), custom_call_target="tpu_custom_call" | custom-call | tf_op jit(solution)/shard_map/pallas_call | solution.py:492

commit v5 on v4

--- a/solution.py
+++ b/solution.py
@@ -23,9 +23,11 @@
 NK = DIM // KC
 CH = 256
 NCH = DIM // CH
-EARLY = 3
 NS = 24
 N1 = NK * NE
+N2 = NCH * NE // 4
+NA = N1 + N2
+NB = NA - NE
 BF16_MAX = 3.3895313892515355e38
 
 
@@ -36,7 +38,7 @@
 def kernel(tok_a, tok_b, e_a, s_a, e_b, s_b, g_a, g_b, sw1, sw3, sw2, rw1, rw3, rw2,
            out_ab, out_kept, out_x,
            ring, sw13, sw2v, tok, ytok, buf, pf, hid, pmat, g3,
-           recvr, recvl, xr, hso, hyo, hsi, ost, mi, mg,
+           recvr, recvl, xr, hsi, mi, mg,
            loc_sem, ring_sem, snd, rcv):
     tp = lax.axis_index('tp')
     ep = lax.axis_index('ep')
@@ -71,7 +73,7 @@
     def put(m, c):
         if c == NCH - 1:
             return local(kept(m, c), out_kept.at[m], 6)
-        return local(ost.at[m, :, out_cols(c)], out_ab.at[m, :, out_cols(c)], 7)
+        return local(ytok.at[part(m, TOK), out_cols(c)], out_ab.at[m, :, out_cols(c)], 7)
 
     def first_item(n, slot):
         e, rows = n % NE, part(n // NE, KC)
@@ -83,31 +85,24 @@
                                       ring.at[slot, pl.ds((i // 2) * FF, FF), pl.ds((i % 2) * CH, CH)],
                                       ring_sem.at[slot]) for i in range(4)]
 
-    def load2(c, slot0):
-        def go(q, _):
-            for d in second_item(c, q, slot0 + q):
-                d.start()
-            return 0
-        lax.fori_loop(0, NE // 4, go, 0)
-
     def wait_item(slot):
         pltpu.make_async_copy(rw1.at[0, pl.ds(0, 2 * KC)], ring.at[slot], ring_sem.at[slot]).wait()
 
+    segments = [(0, N1, first_item, 0), (N1, NA, None, N1), (NA, NB + N1, first_item, NB), (NB + N1, NB + NA, None, NB + N1)]
+
     def refill(n, low, high):
-        def one():
-            for d in first_item(n, n % NS):
-                d.start()
-
-        def two():
-            for d in second_item((n - N1) // 4, (n - N1) % 4, n % NS):
-                d.start()
-        if high <= N1:
-            one()
-        elif low >= N1:
-            two()
-        else:
-            pl.when(n < N1)(one)
-            pl.when(n >= N1)(two)
+        for a, b, kind, zero in segments:
+            if a >= high or b <= low:
+                continue
+
+            def go(kind=kind, zero=zero):
+                i = n - zero
+                for d in (kind(i, n % NS) if kind else second_item(i // 4, i % 4, n % NS)):
+                    d.start()
+            if a <= low and high <= b:
+                go()
+            else:
+                pl.when((n >= a) & (n < b))(go)
 
     def same(ref, sem, dev):
         return remote(ref, ref, sem, dev)
@@ -124,14 +119,14 @@
     half = part(core, FF // 2)
     y_w2 = remote(sw2.at[half], sw2v.at[1, half], 8, dev_y)
     f_w2 = remote(sw2v.at[1, half], sw2v.at[1, half], 9, dev_d)
-    y_hid = remote(hyo, hsi, 10, dev_y)
+    y_hid = remote(buf.at[0, pl.ds(0, 2 * TOK)], hsi, 10, dev_y)
     x_tok, f_tok = [], []
     for k in range(NK):
         cols = part(k, KC)
         x_tok.append([remote(toks[m].at[:, cols], tok.at[2, m, :, cols], 11 + 2 * k + m, dev_x) for m in range(2)])
         f_tok.append([remote(tok.at[2, m, :, cols], tok.at[3, m, :, cols], 11 + 2 * NK + 2 * k + m, dev_d) for m in range(2)])
     base_sem = 11 + 4 * NK
-    loc_of = base_sem + NCH + EARLY
+    loc_of = base_sem + 2 * NCH
 
     def block(kind, m, c):
         return pf.at[m, pl.ds((kind * NCH + c) * TOK, TOK), pl.ds(0, CH)]
@@ -149,12 +144,7 @@
         return block(3, m, c)
 
     def d_rem(m, c):
-        return remote(send_r(m, c), recvr.at[m, :, out_cols(c)], base_sem + (2 * c + m if c < EARLY else c + EARLY), dev_d)
-
-    def d_rem_all(c, ms):
-        if len(ms) == 1:
-            return d_rem(ms[0], c)
-        return same(recvr.at[:, :, out_cols(c)], base_sem + c + EARLY, dev_d)
+        return remote(send_r(m, c), recvr.at[m, :, out_cols(c)], base_sem + 2 * c + m, dev_d)
 
     def d_loc(m, c):
         return remote(send_l(m, c), recvl.at[m, :, out_cols(c)], loc_of, dev_d)
@@ -163,11 +153,13 @@
 
     def x_part(m, c):
         to = out_x.at[m] if c == NCH - 1 else xr.at[m, :, out_cols(c)]
-        return remote(send_x(m, c), to, loc_of + 1 + max(c - (NCH - 3), 0), dev_x)
-
-    x_part_all = [same(xr.at[:, :, pl.ds(0, (NCH - 2) * CH)], loc_of + 1, dev_x),
-                  same(xr.at[:, :, out_cols(NCH - 2)], loc_of + 2, dev_x),
-                  same(out_x, loc_of + 3, dev_x)]
+        group = 3 if c == NCH - 1 else (0 if m == 0 else max(c - (NCH - 4), 1))
+        return remote(send_x(m, c), to, loc_of + 1 + group, dev_x)
+
+    x_part_all = [same(xr.at[0, :, pl.ds(0, (NCH - 1) * CH)], loc_of + 1, dev_x),
+                  same(xr.at[1, :, pl.ds(0, (NCH - 2) * CH)], loc_of + 2, dev_x),
+                  same(xr.at[1, :, out_cols(NCH - 2)], loc_of + 3, dev_x),
+                  same(out_x, loc_of + 4, dev_x)]
 
     def swiglu(rows, w1, w3):
         p1 = dot(rows, w1)
@@ -213,16 +205,16 @@
     def load(ref, ms, at):
         return jnp.concatenate([ref[m, at, :] for m in ms], axis=0) if len(ms) > 1 else ref[ms[0], at, :]
 
-    def stage1(k, ms, half=None, fresh=True, done=True):
-        per = 8 if k < NK - 1 else 16
+    def stage1(k, ms, half=None):
+        per = 4 if len(ms) > 1 else 8
+        item0 = k * NE if 0 in ms else NB + k * NE
 
         def step(i, _):
-            if fresh:
-                for u in range(per):
-                    wait_item((k * NE + per * i + u) % NS)
+            for u in range(per):
+                wait_item((item0 + per * i + u) % NS)
             for u in range(per):
                 e = per * i + u
-                slot = (k * NE + e) % NS
+                slot = (item0 + e) % NS
                 rows = load(buf, ms, part(e, ROWS))
                 p1 = dot(rows, ring[slot, :KC])
                 p3 = dot(rows, ring[slot, KC:])
@@ -239,11 +231,9 @@
                         pf[m, at3, :] = p3[at]
                     else:
                         hid[m, e] = p1[at]
-            if done:
-                for u in range(per):
-                    low = k * NE + NS if half is None else k * NE + NS + half * NE // 2
-                    high = (k + 1) * NE + NS if half is None else low + NE // 2
-                    refill(k * NE + per * i + u + NS, low, high)
+            for u in range(per):
+                low = item0 + NS + (half or 0) * NE // 2
+                refill(item0 + per * i + u + NS, low, low + (NE if half is None else NE // 2))
             return 0
         if half is None:
             lax.fori_loop(0, NE // per, step, 0)
@@ -254,49 +244,42 @@
         q = dot(g3[SRC * m + s], buf[m, s * SROWS:(s + 1) * SROWS, :CH])
         return q[:TOK] + q[TOK:2 * TOK] + q[2 * TOK:]
 
-    def stage2(c, ms, slot0, fresh=True):
-        loop = 2 if len(ms) > 1 else 4
-
-        def step(q, _):
-            r = []
-            if fresh:
-                for i in range(loop):
-                    wait_item(slot0 + q * loop + i)
-            for i in range(4 * loop):
-                slot = slot0 + q * loop + i // 4
-                a, b = (i % 4 // 2) * FF, (i % 2) * CH
-                e = 4 * loop * q + i
-                rows = jnp.concatenate([hid[m, e] for m in ms], axis=0) if len(ms) > 1 else hid[ms[0], e]
-                r.append(dot(rows, ring[slot, a:a + FF, b:b + CH]))
-            for j, m in enumerate(ms):
+    def stage2(c, m):
+        item0 = N1 + c * NE // 4 if m == 0 else NB + N1 + c * NE // 4
+        for q in range(NE // 4):
+            wait_item((item0 + q) % NS)
+
+        def step(_, unused):
+            for q in range(NE // 4):
+                r = []
+                for e in range(4):
+                    a, b = (e // 2) * FF, (e % 2) * CH
+                    r.append(dot(hid[m, 4 * q + e], ring[(item0 + q) % NS, a:a + FF, b:b + CH]))
                 for s in range(SRC):
-                    low = j * ROWS + s * CAP
-                    rows = jnp.concatenate([v[low:low + CAP] for v in r], axis=0)
-                    k = 4 * CAP * loop
-                    buf[m, pl.ds(pl.multiple_of(s * SROWS + q * k, 2 * CAP), k), :CH] = rows.astype(BF16)
+                    rows = jnp.concatenate([v[s * CAP:(s + 1) * CAP] for v in r], axis=0)
+                    buf[m, s * SROWS + 4 * q * CAP:s * SROWS + 4 * (q + 1) * CAP, :CH] = rows.astype(BF16)
             return 0
-        lax.fori_loop(0, 4 // loop, step, 0)
-
-        to_die = [combine(m, 3) for m in ms]
-        to_x = [combine(m, 2) for m in ms]
-        for m, v in zip(ms, to_die):
-            send_r(m, c)[...] = v
-            d_rem(m, c).start()
-        for m, v in zip(ms, to_x):
-            send_x(m, c)[...] = v
-        to_die = [combine(m, 1) for m in ms]
-        home = [combine(m, 0) for m in ms]
-        for m, v in zip(ms, to_die):
-            send_l(m, c)[...] = v
-            d_loc(m, c).start()
-        for m, v in zip(ms, home):
-            kept(m, c)[...] = v
-
-    def pass_on(c, ms):
-        d_rem_all(c, ms).wait_recv()
-        for m in ms:
-            send_x(m, c)[...] = send_x(m, c)[...] + recvr[m, :, c * CH:(c + 1) * CH]
-            x_part(m, c).start()
+        lax.fori_loop(0, 1, step, 0)
+
+        def more(q, _):
+            refill(item0 + q + NS, item0 + NS, item0 + NS + NE // 4)
+            return 0
+        lax.fori_loop(0, NE // 4, more, 0)
+
+    def sums(c, m):
+        to_die, to_x = combine(m, 3), combine(m, 2)
+        send_r(m, c)[...] = to_die
+        d_rem(m, c).start()
+        send_x(m, c)[...] = to_x
+        to_die, home = combine(m, 1), combine(m, 0)
+        send_l(m, c)[...] = to_die
+        d_loc(m, c).start()
+        kept(m, c)[...] = home
+
+    def pass_on(c, m):
+        d_rem(m, c).wait_recv()
+        send_x(m, c)[...] = send_x(m, c)[...] + recvr[m, :, c * CH:(c + 1) * CH]
+        x_part(m, c).start()
 
     def arrived(k, ms):
         for m in ms:
@@ -315,7 +298,7 @@
         return 0
     lax.fori_loop(0, 8, fill, 0)
     pl.semaphore_wait(barrier, 3)
-    for c in x_meta + d_meta + x_tok[0] + d_tok + x_tok[1] + x_tok[2] + y_tok + [y_w2]:
+    for c in x_meta + d_meta + x_tok[0] + d_tok + [x_tok[k][m] for m in range(2) for k in range(1, NK)] + y_tok + [y_w2]:
         c.start()
     lax.fori_loop(8, NS, fill, 0)
     for c in own_all:
@@ -340,60 +323,56 @@
     for m in both:
         f_tok[0][m].wait_recv()
         dispatch(0, m, 1)
-    stage1(0, both)
+    stage1(0, both, half=0)
     arrived(1, a)
+    stage1(0, both, half=1)
     dispatch(1, 0, 0)
-    arrived(1, b)
-    dispatch(1, 1, 0)
-    for m in both:
-        f_tok[1][m].wait_recv()
-        dispatch(1, m, 1)
-    stage1(1, both, half=0)
+    f_tok[1][0].wait_recv()
+    dispatch(1, 0, 1)
+    stage1(1, a, half=0)
     arrived(2, a)
-    stage1(1, both, half=1)
+    stage1(1, a, half=1)
     dispatch(2, 0, 0)
     f_tok[2][0].wait_recv()
     dispatch(2, 0, 1)
-    stage1(2, a, done=False)
-    arrived(2, b)
-
-    stage2(0, a, 0)
-    load2(2, 0)
+    arrived(1, b)
+    stage1(2, a)
+    for c in range(NCH):
+        stage2(c, 0)
+        if c:
+            pass_on(c - 1, 0)
+        sums(c, 0)
+        if c == 0:
+            dispatch(1, 1, 0)
+            f_tok[1][1].wait_recv()
+        if c == 2:
+            arrived(2, b)
+            dispatch(1, 1, 1)
+
+    stage1(1, b)
+    pass_on(NCH - 1, 0)
     dispatch(2, 1, 0)
-    pass_on(0, a)
-    stage2(1, a, 4)
     f_tok[2][1].wait_recv()
     dispatch(2, 1, 1)
-    pass_on(1, a)
-    stage2(2, a, 0)
+    stage1(2, b)
     for c in shared:
         c.start()
-    pass_on(2, a)
-    stage1(2, b, fresh=False, done=False)
-    load2(0, 8)
-    load2(3, 12)
-    load2(4, 16)
-    load2(5, 20)
-    stage2(1, b, 4, fresh=False)
-    pass_on(1, b)
-    stage2(2, b, 0, fresh=False)
-    pass_on(2, b)
-    stage2(0, b, 8)
-    pass_on(0, b)
-    stage2(3, both, 12)
-    pass_on(3, both)
-    for c in shared:
-        c.wait()
-    y_tok_all.wait_recv()
+    for c in range(NCH):
+        stage2(c, 1)
+        if c:
+            pass_on(c - 1, 1)
+        sums(c, 1)
+        if c == NCH - 1:
+            pass_on(c, 1)
+        if c == 3:
+            for d in shared:
+                d.wait()
+            y_tok_all.wait_recv()
+            for m in both:
+                buf[0, m * TOK:(m + 1) * TOK, :] = swiglu(ytok[m * TOK:(m + 1) * TOK], sw13[0], sw13[1])
+            y_hid.start()
     for m in both:
-        hyo[m] = swiglu(ytok[m * TOK:(m + 1) * TOK], sw13[0], sw13[1])
-    y_hid.start()
-    stage2(4, both, 16)
-    pass_on(4, both)
-    stage2(5, both, 20)
-    pass_on(5, both)
-    for m in both:
-        hso[m] = swiglu(tok[0, m], sw13[0], sw13[1])
+        buf[0, (2 + m) * TOK:(3 + m) * TOK, :] = swiglu(tok[0, m], sw13[0], sw13[1])
     y_w2.wait_recv()
     f_w2.start()
     y_hid.wait_recv()
@@ -403,16 +382,18 @@
     for c in range(NCH - 1, -1, -1):
         at = slice(c * CH, (c + 1) * CH)
         for m in both:
-            s = dot(hso[m], sw2v[0, :, at]) + dot(hsi[m], sw2v[1, :, at])
+            s = dot(buf[0, (2 + m) * TOK:(3 + m) * TOK, :], sw2v[0, :, at]) + dot(hsi[m * TOK:(m + 1) * TOK, :], sw2v[1, :, at])
             kept(m, c)[...] = kept(m, c)[...] + recvl[m, :, at] + s + tok[0, m, :, at].astype(F32)
             if c == NCH - 1:
                 put(m, c).start()
-    for c in range(NCH - 1):
-        at = slice(c * CH, (c + 1) * CH)
-        if c == 0 or c == NCH - 2:
-            x_part_all[min(c, 1)].wait_recv()
-        for m in both:
-            ost[m, :, at] = (kept(m, c)[...] + xr[m, :, at]).astype(BF16)
+    for m in both:
+        for c in range(NCH - 1):
+            at = slice(c * CH, (c + 1) * CH)
+            if c == 0:
+                x_part_all[m].wait_recv()
+            if m == 1 and c == NCH - 2:
+                x_part_all[2].wait_recv()
+            ytok[m * TOK:(m + 1) * TOK, at] = (kept(m, c)[...] + xr[m, :, at]).astype(BF16)
             put(m, c).start()
 
     for c in x_meta_all + d_meta_all + f_meta + [d_tok_all, y_tok_all, y_w2, f_w2, y_hid, d_loc_all]:
@@ -420,11 +401,11 @@
     for c in sum(x_tok, []) + sum(f_tok, []) + x_part_all:
         c.wait_send()
     for c in range(NCH):
-        for ms in ((both,) if c >= EARLY else (a, b)):
-            d_rem_all(c, ms).wait_send()
+        for m in both:
+            d_rem(m, c).wait_send()
     local(recvl.at[:, :, out_cols(NCH - 1)], out_kept, 6).wait()
-    local(ost.at[:, :, pl.ds(0, DIM - CH)], out_ab.at[:, :, pl.ds(0, DIM - CH)], 7).wait()
-    x_part_all[2].wait_recv()
+    local(tok.at[0, :, :, pl.ds(0, DIM - CH)], out_ab.at[:, :, pl.ds(0, DIM - CH)], 7).wait()
+    x_part_all[3].wait_recv()
 
 
 def finish(most, kept, x, out_a, out_b, row, k_v, x_v, sem):
@@ -450,7 +431,7 @@
 def solution(mesh):
     tok_spec = P(('data', 'ep', 'tp'), None)
     in_specs = (tok_spec,) * 8 + (P(None, 'tp'), P(None, 'tp'), P('tp', None), P('ep', None, None), P('ep', None, None), P('ep', None, None))
-    nsem = 11 + 4 * NK + NCH + EARLY + 4
+    nsem = 11 + 4 * NK + 2 * NCH + 5
     scratch = [
         pltpu.VMEM((NS, 2 * KC, FF), BF16),
         pltpu.VMEM((2, DIM, FF), BF16),
@@ -464,11 +445,8 @@
         pltpu.VMEM((2 * SRC, 3 * TOK, SROWS), BF16),
         pltpu.VMEM((2, TOK, DIM), F32),
         pltpu.VMEM((2, TOK, DIM), F32),
-        pltpu.VMEM((2, TOK, DIM), F32),
-        pltpu.VMEM((2, TOK, FF), BF16),
-        pltpu.VMEM((2, TOK, FF), BF16),
-        pltpu.VMEM((2, TOK, FF), BF16),
-        pltpu.VMEM((2, TOK, DIM), BF16),
+        pltpu.VMEM((2, TOK, DIM - CH), F32),
+        pltpu.VMEM((2 * TOK, FF), BF16),
         pltpu.VMEM((4, 4, TOPK, TOK), jnp.int32),
         pltpu.VMEM((4, 2, TOPK, TOK), F32),
         pltpu.SemaphoreType.DMA((8,)),

time: 69.9 us -> 68 us (0.973)
  Pallas kernels: 69 us -> 67 us
    pallas_call x1, Pallas kernels: 66.8 us -> 64.9 us  [layer_local(): pl.pallas_call(kernel, out_shape=(jax.ShapeDtypeStruct((2, TOK, DIM), BF1...]
where the time goes in v5:
time: 68 us; the launch traced here: 67.8 us
  Pallas kernels  67 us (99%)
  between operations  0.8 us (1%)
    pallas_call x1, Pallas kernels, layer_local(): pl.pallas_call(kernel, out_shape=(jax.ShapeDtypeStruct((2, TOK, DIM), BF1...  64.9 us
    pallas_call x1, Pallas kernels, layer_local(): pl.pallas_call(finish, out_shape=(jax.ShapeDtypeStruct((TOK, DIM), BF16),...  2.18 us

profile of v5, /device:TPU:0, one launch (start us, length us, event | category | flops | bytes accessed | tf_op | source)
XLA Modules:
  0.0 67.8 jit_solution(12183370821945290992)
XLA Ops:
  0.6 64.9 %shard_map.149 = (bf16[2,128,1536]{2,1,0:T(8,128)(2,1)}, f32[2,128,256]{2,1,0:T(8,128)}, f32[2,128,256]{2,1,0:T(8,128)}) custom-call(bf16[128,1536]{1,0:T(8,128)(2,1)} %tok_a.1, bf16[128,1536]{1,0:T(8,128)(2,1)} %tok_b.1, s32[6,128]{1,0:T(8,128)} %bitcast.6, s32[6,128]{1,0:T(8,128)} %bitcast.7, s32[6,128]{1,0:T(8,128)} %bitcast.8, s32[6,128]{1,0:T(8,128)} %bitcast.9, ...), custom_call_target="tpu_custom_call" | custom-call | tf_op jit(solution)/shard_map/pallas_call | solution.py:461
  65.5 2.2 %shard_map.150 = (bf16[128,1536]{1,0:T(8,128)(2,1)}, bf16[128,1536]{1,0:T(8,128)(2,1)}) custom-call(bf16[2,128,1536]{2,1,0:T(8,128)(2,1)} %get-tuple-element.5.most, f32[2,128,256]{2,1,0:T(8,128)} %get-tuple-element.6.kept, f32[2,128,256]{2,1,0:T(8,128)} %get-tuple-element.7.x), custom_call_target="tpu_custom_call" | custom-call | tf_op jit(solution)/shard_map/pallas_call | solution.py:470

commit v6 on v5

--- a/solution.py
+++ b/solution.py
@@ -37,7 +37,7 @@
 
 def kernel(tok_a, tok_b, e_a, s_a, e_b, s_b, g_a, g_b, sw1, sw3, sw2, rw1, rw3, rw2,
            out_ab, out_kept, out_x,
-           ring, sw13, sw2v, tok, ytok, buf, pf, hid, pmat, g3,
+           ring, sw13, sw2v, tok, ytok, buf, pf, hid, g3,
            recvr, recvl, xr, hsi, mi, mg,
            loc_sem, ring_sem, snd, rcv):
     tp = lax.axis_index('tp')
@@ -52,8 +52,8 @@
     def local(src, dst, sem):
         return pltpu.make_async_copy(src, dst, loc_sem.at[sem])
 
-    def remote(src, dst, sem, dev):
-        return pltpu.make_async_remote_copy(src_ref=src, dst_ref=dst, send_sem=snd.at[sem], recv_sem=rcv.at[sem],
+    def remote(src, dst, sem, dev, kind):
+        return pltpu.make_async_remote_copy(src_ref=src, dst_ref=dst, send_sem=snd.at[kind], recv_sem=rcv.at[sem],
                                             device_id=dev, device_id_type=MESH)
 
     def mult(i, k):
@@ -77,16 +77,17 @@
 
     def first_item(n, slot):
         e, rows = n % NE, part(n // NE, KC)
-        return (pltpu.make_async_copy(rw1.at[e, rows], ring.at[slot, pl.ds(0, KC)], ring_sem.at[slot]),
-                pltpu.make_async_copy(rw3.at[e, rows], ring.at[slot, pl.ds(KC, KC)], ring_sem.at[slot]))
+        return (pltpu.make_async_copy(rw1.at[e, rows], ring.at[slot, pl.ds(0, KC)], ring_sem.at[slot // 4]),
+                pltpu.make_async_copy(rw3.at[e, rows], ring.at[slot, pl.ds(KC, KC)], ring_sem.at[slot // 4]))
 
     def second_item(c, q, slot):
         return [pltpu.make_async_copy(rw2.at[4 * q + i, :, out_cols(c)],
                                       ring.at[slot, pl.ds((i // 2) * FF, FF), pl.ds((i % 2) * CH, CH)],
-                                      ring_sem.at[slot]) for i in range(4)]
-
-    def wait_item(slot):
-        pltpu.make_async_copy(rw1.at[0, pl.ds(0, 2 * KC)], ring.at[slot], ring_sem.at[slot]).wait()
+                                      ring_sem.at[slot // 4]) for i in range(4)]
+
+    def wait_items(n):
+        slot = n % NS
+        pltpu.make_async_copy(rw1.at[pl.ds(0, 4), pl.ds(0, 2 * KC)], ring.at[part(slot // 4, 4)], ring_sem.at[slot // 4]).wait()
 
     segments = [(0, N1, first_item, 0), (N1, NA, None, N1), (NA, NB + N1, first_item, NB), (NB + N1, NB + NA, None, NB + N1)]
 
@@ -104,27 +105,27 @@
             else:
                 pl.when((n >= a) & (n < b))(go)
 
-    def same(ref, sem, dev):
-        return remote(ref, ref, sem, dev)
-
-    d_meta = [remote(ids[i], mi.at[1, i], 0, dev_d) for i in range(4)] + [remote(gates[m], mg.at[1, m], 1, dev_d) for m in range(2)]
-    d_meta_all = [same(mi.at[1], 0, dev_d), same(mg.at[1], 1, dev_d)]
-    x_meta = [remote(ids[i], mi.at[2, i], 2, dev_x) for i in range(4)] + [remote(gates[m], mg.at[2, m], 3, dev_x) for m in range(2)]
-    x_meta_all = [same(mi.at[2], 2, dev_x), same(mg.at[2], 3, dev_x)]
-    f_meta = [remote(mi.at[2], mi.at[3], 4, dev_d), remote(mg.at[2], mg.at[3], 5, dev_d)]
-    d_tok = [remote(toks[m], tok.at[1, m], 6, dev_d) for m in range(2)]
-    d_tok_all = same(tok.at[1], 6, dev_d)
-    y_tok = [remote(toks[m], ytok.at[pl.ds(m * TOK, TOK)], 7, dev_y) for m in range(2)]
-    y_tok_all = same(ytok, 7, dev_y)
+    def same(ref, sem, dev, kind):
+        return remote(ref, ref, sem, dev, kind)
+
+    d_meta = [remote(ids[i], mi.at[1, i], 0, dev_d, 1) for i in range(4)] + [remote(gates[m], mg.at[1, m], 1, dev_d, 2) for m in range(2)]
+    d_meta_all = [same(mi.at[1], 0, dev_d, 1), same(mg.at[1], 1, dev_d, 2)]
+    x_meta = [remote(ids[i], mi.at[2, i], 2, dev_x, 1) for i in range(4)] + [remote(gates[m], mg.at[2, m], 3, dev_x, 2) for m in range(2)]
+    x_meta_all = [same(mi.at[2], 2, dev_x, 1), same(mg.at[2], 3, dev_x, 2)]
+    f_meta = [remote(mi.at[2], mi.at[3], 4, dev_d, 1), remote(mg.at[2], mg.at[3], 5, dev_d, 2)]
+    d_tok = [remote(toks[m], tok.at[1, m], 6, dev_d, 0) for m in range(2)]
+    d_tok_all = same(tok.at[1], 6, dev_d, 0)
+    y_tok = [remote(toks[m], ytok.at[pl.ds(m * TOK, TOK)], 7, dev_y, 0) for m in range(2)]
+    y_tok_all = same(ytok, 7, dev_y, 0)
     half = part(core, FF // 2)
-    y_w2 = remote(sw2.at[half], sw2v.at[1, half], 8, dev_y)
-    f_w2 = remote(sw2v.at[1, half], sw2v.at[1, half], 9, dev_d)
-    y_hid = remote(buf.at[0, pl.ds(0, 2 * TOK)], hsi, 10, dev_y)
+    y_w2 = remote(sw2.at[half], sw2v.at[1, half], 8, dev_y, 3)
+    f_w2 = remote(sw2v.at[1, half], sw2v.at[1, half], 9, dev_d, 3)
+    y_hid = remote(buf.at[0, pl.ds(0, 2 * TOK)], hsi, 10, dev_y, 4)
     x_tok, f_tok = [], []
     for k in range(NK):
         cols = part(k, KC)
-        x_tok.append([remote(toks[m].at[:, cols], tok.at[2, m, :, cols], 11 + 2 * k + m, dev_x) for m in range(2)])
-        f_tok.append([remote(tok.at[2, m, :, cols], tok.at[3, m, :, cols], 11 + 2 * NK + 2 * k + m, dev_d) for m in range(2)])
+        x_tok.append([remote(toks[m].at[:, cols], tok.at[2, m, :, cols], 11 + 2 * k + m, dev_x, 0) for m in range(2)])
+        f_tok.append([remote(tok.at[2, m, :, cols], tok.at[3, m, :, cols], 11 + 2 * NK + 2 * k + m, dev_d, 0) for m in range(2)])
     base_sem = 11 + 4 * NK
     loc_of = base_sem + 2 * NCH
 
@@ -144,22 +145,22 @@
         return block(3, m, c)
 
     def d_rem(m, c):
-        return remote(send_r(m, c), recvr.at[m, :, out_cols(c)], base_sem + 2 * c + m, dev_d)
+        return remote(send_r(m, c), recvr.at[m, :, out_cols(c)], base_sem + 2 * c + m, dev_d, 5)
 
     def d_loc(m, c):
-        return remote(send_l(m, c), recvl.at[m, :, out_cols(c)], loc_of, dev_d)
-
-    d_loc_all = same(recvl, loc_of, dev_d)
+        return remote(send_l(m, c), recvl.at[m, :, out_cols(c)], loc_of, dev_d, 6)
+
+    d_loc_all = same(recvl, loc_of, dev_d, 6)
 
     def x_part(m, c):
         to = out_x.at[m] if c == NCH - 1 else xr.at[m, :, out_cols(c)]
         group = 3 if c == NCH - 1 else (0 if m == 0 else max(c - (NCH - 4), 1))
-        return remote(send_x(m, c), to, loc_of + 1 + group, dev_x)
-
-    x_part_all = [same(xr.at[0, :, pl.ds(0, (NCH - 1) * CH)], loc_of + 1, dev_x),
-                  same(xr.at[1, :, pl.ds(0, (NCH - 2) * CH)], loc_of + 2, dev_x),
-                  same(xr.at[1, :, out_cols(NCH - 2)], loc_of + 3, dev_x),
-                  same(out_x, loc_of + 4, dev_x)]
+        return remote(send_x(m, c), to, loc_of + 1 + group, dev_x, 7)
+
+    x_part_all = [same(xr.at[0, :, pl.ds(0, (NCH - 1) * CH)], loc_of + 1, dev_x, 7),
+                  same(xr.at[1, :, pl.ds(0, (NCH - 2) * CH)], loc_of + 2, dev_x, 7),
+                  same(xr.at[1, :, out_cols(NCH - 2)], loc_of + 3, dev_x, 7),
+                  same(out_x, loc_of + 4, dev_x, 7)]
 
     def swiglu(rows, w1, w3):
         p1 = dot(rows, w1)
@@ -182,7 +183,7 @@
                 same = row == rid[j:j + 1, :]
                 hit = jnp.where(same, 1.0, hit)
                 gt = jnp.where(same, g[j:j + 1, :], gt)
-            pmat[SRC * m + src, at, :] = hit.astype(BF16)
+            hid[1, part(src * (SROWS // 128) + b, 128), part(m, TOK)] = hit.astype(BF16)
             gg = gt.T
             hi = jnp.minimum(gg, BF16_MAX).astype(BF16)
             r1 = gg - hi.astype(F32)
@@ -195,8 +196,9 @@
 
     def dispatch(k, m, pair):
         cols = part(k, KC)
-        r0 = dot(pmat[SRC * m + 2 * pair], tok[2 * pair, m, :, cols])
-        r1 = dot(pmat[SRC * m + 2 * pair + 1], tok[2 * pair + 1, m, :, cols])
+        place = [hid[1, s * SROWS:(s + 1) * SROWS, m * TOK:(m + 1) * TOK] for s in (2 * pair, 2 * pair + 1)]
+        r0 = dot(place[0], tok[2 * pair, m, :, cols])
+        r1 = dot(place[1], tok[2 * pair + 1, m, :, cols])
         for e in range(NE):
             both = jnp.concatenate([r0[e * CAP:(e + 1) * CAP], r1[e * CAP:(e + 1) * CAP]], axis=0)
             at = e * ROWS + pair * 2 * CAP
@@ -206,12 +208,12 @@
         return jnp.concatenate([ref[m, at, :] for m in ms], axis=0) if len(ms) > 1 else ref[ms[0], at, :]
 
     def stage1(k, ms, half=None):
-        per = 4 if len(ms) > 1 else 8
+        per = 8
         item0 = k * NE if 0 in ms else NB + k * NE
 
         def step(i, _):
-            for u in range(per):
-                wait_item((item0 + per * i + u) % NS)
+            for u in range(0, per, 4):
+                wait_items(item0 + per * i + u)
             for u in range(per):
                 e = per * i + u
                 slot = (item0 + e) % NS
@@ -230,7 +232,7 @@
                         pf[m, at1, :] = p1[at]
                         pf[m, at3, :] = p3[at]
                     else:
-                        hid[m, e] = p1[at]
+                        hid[m, part(e, ROWS), :] = p1[at]
             for u in range(per):
                 low = item0 + NS + (half or 0) * NE // 2
                 refill(item0 + per * i + u + NS, low, low + (NE if half is None else NE // 2))
@@ -246,15 +248,14 @@
 
     def stage2(c, m):
         item0 = N1 + c * NE // 4 if m == 0 else NB + N1 + c * NE // 4
-        for q in range(NE // 4):
-            wait_item((item0 + q) % NS)
+        wait_items(item0)
 
         def step(_, unused):
             for q in range(NE // 4):
                 r = []
                 for e in range(4):
                     a, b = (e // 2) * FF, (e % 2) * CH
-                    r.append(dot(hid[m, 4 * q + e], ring[(item0 + q) % NS, a:a + FF, b:b + CH]))
+                    r.append(dot(hid[m, part(4 * q + e, ROWS), :], ring[(item0 + q) % NS, a:a + FF, b:b + CH]))
                 for s in range(SRC):
                     rows = jnp.concatenate([v[s * CAP:(s + 1) * CAP] for v in r], axis=0)
                     buf[m, s * SROWS + 4 * q * CAP:s * SROWS + 4 * (q + 1) * CAP, :CH] = rows.astype(BF16)
@@ -268,11 +269,14 @@
 
     def sums(c, m):
         to_die, to_x = combine(m, 3), combine(m, 2)
+        if c:
+            die_own, home = combine(m, 1), combine(m, 0)
         send_r(m, c)[...] = to_die
         d_rem(m, c).start()
         send_x(m, c)[...] = to_x
-        to_die, home = combine(m, 1), combine(m, 0)
-        send_l(m, c)[...] = to_die
+        if not c:
+            die_own, home = combine(m, 1), combine(m, 0)
+        send_l(m, c)[...] = die_own
         d_loc(m, c).start()
         kept(m, c)[...] = home
 
@@ -396,13 +400,8 @@
             ytok[m * TOK:(m + 1) * TOK, at] = (kept(m, c)[...] + xr[m, :, at]).astype(BF16)
             put(m, c).start()
 
-    for c in x_meta_all + d_meta_all + f_meta + [d_tok_all, y_tok_all, y_w2, f_w2, y_hid, d_loc_all]:
-        c.wait_send()
-    for c in sum(x_tok, []) + sum(f_tok, []) + x_part_all:
-        c.wait_send()
-    for c in range(NCH):
-        for m in both:
-            d_rem(m, c).wait_send()
+    for kind, ref in enumerate((tok, mi.at[pl.ds(0, 3)], mg.at[pl.ds(0, 3)], sw2v.at[1], hsi, recvr, recvl, recvr)):
+        same(ref, 0, dev_d, kind).wait_send()
     local(recvl.at[:, :, out_cols(NCH - 1)], out_kept, 6).wait()
     local(tok.at[0, :, :, pl.ds(0, DIM - CH)], out_ab.at[:, :, pl.ds(0, DIM - CH)], 7).wait()
     x_part_all[3].wait_recv()
@@ -440,8 +439,7 @@
         pltpu.VMEM((2 * TOK, DIM), BF16),
         pltpu.VMEM((2, NE * ROWS, KC), BF16),
         pltpu.VMEM((2, 2 * NE * ROWS, FF), F32),
-        pltpu.VMEM((2, NE, ROWS, FF), BF16),
-        pltpu.VMEM((2 * SRC, SROWS, TOK), BF16),
+        pltpu.VMEM((2, NE * ROWS, FF), BF16),
         pltpu.VMEM((2 * SRC, 3 * TOK, SROWS), BF16),
         pltpu.VMEM((2, TOK, DIM), F32),
         pltpu.VMEM((2, TOK, DIM), F32),
@@ -450,8 +448,8 @@
         pltpu.VMEM((4, 4, TOPK, TOK), jnp.int32),
         pltpu.VMEM((4, 2, TOPK, TOK), F32),
         pltpu.SemaphoreType.DMA((8,)),
-        pltpu.SemaphoreType.DMA((NS,)),
-        pltpu.SemaphoreType.DMA((nsem,)),
+        pltpu.SemaphoreType.DMA((NS // 4,)),
+        pltpu.SemaphoreType.DMA((8,)),
         pltpu.SemaphoreType.DMA((nsem,)),
     ]
 

time: 68 us -> 67.2 us (0.988)
  Pallas kernels: 67 us -> 66.3 us
    pallas_call x1, Pallas kernels: 64.9 us -> 64.1 us  [layer_local(): pl.pallas_call(kernel, out_shape=(jax.ShapeDtypeStruct((2, TOK, DIM), BF1...]
where the time goes in v6:
time: 67.2 us; the launch traced here: 67.1 us
  Pallas kernels  66.3 us (99%)
  between operations  0.82 us (1%)
    pallas_call x1, Pallas kernels, layer_local(): pl.pallas_call(kernel, out_shape=(jax.ShapeDtypeStruct((2, TOK, DIM), BF1...  64.1 us
    pallas_call x1, Pallas kernels, layer_local(): pl.pallas_call(finish, out_shape=(jax.ShapeDtypeStruct((TOK, DIM), BF16),...  2.18 us

profile of v6, /device:TPU:0, one launch (start us, length us, event | category | flops | bytes accessed | tf_op | source)
XLA Modules:
  0.0 67.1 jit_solution(16828646844964628364)
XLA Ops:
  0.6 64.1 %shard_map.149 = (bf16[2,128,1536]{2,1,0:T(8,128)(2,1)}, f32[2,128,256]{2,1,0:T(8,128)}, f32[2,128,256]{2,1,0:T(8,128)}) custom-call(bf16[128,1536]{1,0:T(8,128)(2,1)} %tok_a.1, bf16[128,1536]{1,0:T(8,128)(2,1)} %tok_b.1, s32[6,128]{1,0:T(8,128)} %bitcast.6, s32[6,128]{1,0:T(8,128)} %bitcast.7, s32[6,128]{1,0:T(8,128)} %bitcast.8, s32[6,128]{1,0:T(8,128)} %bitcast.9, ...), custom_call_target="tpu_custom_call" | custom-call | tf_op jit(solution)/shard_map/pallas_call | solution.py:459
  64.7 2.2 %shard_map.150 = (bf16[128,1536]{1,0:T(8,128)(2,1)}, bf16[128,1536]{1,0:T(8,128)(2,1)}) custom-call(bf16[2,128,1536]{2,1,0:T(8,128)(2,1)} %get-tuple-element.5.most, f32[2,128,256]{2,1,0:T(8,128)} %get-tuple-element.6.kept, f32[2,128,256]{2,1,0:T(8,128)} %get-tuple-element.7.x), custom_call_target="tpu_custom_call" | custom-call | tf_op jit(solution)/shard_map/pallas_call | solution.py:468
